TPU v7x, 8 devices: a whole 2x2x1 slice. The times are simulated.
8 devices in a mesh: dp: 2 (over z, y), ep: 4 (over x, core).
Axes of the slice: x: 2, y: 2, z: 1, core: 2. Of those that a mesh axis runs over, the one named last changes fastest.
Arguments:
- tok_x: bfloat16 [8192, 4096], P(('dp', 'ep'))
- tok_dy: bfloat16 [8192, 4096], P(('dp', 'ep'))
- exp_first: int32 [8192], P(('dp', 'ep'))
- exp_second: int32 [8192], P(('dp', 'ep'))
- eligible: int32 [8192, 16], P(('dp', 'ep'))
- slot_first: int32 [8192], P(('dp', 'ep'))
- slot_second: int32 [8192], P(('dp', 'ep'))
- ln_weight: bfloat16 [4096], replicated
- ln_bias: bfloat16 [4096], replicated
- router: bfloat16 [4096, 16], replicated
- w_gate: bfloat16 [16, 4096, 960], P('ep')
- w_up: bfloat16 [16, 4096, 960], P('ep')
- w_down: bfloat16 [16, 960, 4096], P('ep')
Outputs:
- output 1: bfloat16 [8192, 4096], P(('dp', 'ep'))
- output 2: bfloat16 [8192, 4096], P(('dp', 'ep'))
- output 3: float32 [16, 4096, 960], P('ep')
- output 4: float32 [16, 4096, 960], P('ep')
- output 5: float32 [16, 960, 4096], P('ep')
- output 6: float32 [4096, 16], replicated
- output 7: float32 [4096], replicated
- output 8: float32 [4096], replicated
All inputs are finite; a program needn't handle non-finite values.
Results may differ from a plain program's by a relative error of at most 0.00516369.
Values are sent between devices in bfloat16 or wider.
A program may use at most 1.25 GiB of HBM per device.

v0:
```python
import jax
import jax.numpy as jnp
from jax import lax
from jax.sharding import PartitionSpec as P

LN_EPS = 1e-5


def layer_norm(x_rows, ln_weight, ln_bias):
    x_float = x_rows.astype(jnp.float32)
    centered = x_float - jnp.mean(x_float, axis=-1, keepdims=True)
    inv_std = lax.rsqrt(jnp.mean(centered * centered, axis=-1, keepdims=True) + LN_EPS)
    x_hat = centered * inv_std
    hidden = (x_hat * ln_weight.astype(jnp.float32) + ln_bias.astype(jnp.float32)).astype(jnp.bfloat16)
    return hidden, x_hat, inv_std


def layer_norm_back(grad_h, x_hat, inv_std, ln_weight):
    scaled = grad_h * ln_weight.astype(jnp.float32)
    return inv_std * (scaled - jnp.mean(scaled, axis=-1, keepdims=True)
                      - x_hat * jnp.mean(scaled * x_hat, axis=-1, keepdims=True))


def masked_gate(logits, allowed, choice):
    expert_ids = jnp.arange(logits.shape[-1])
    prob_all = jax.nn.softmax(jnp.where(allowed, logits, -1e30), axis=-1)
    picked = (choice[:, None] == expert_ids[None, :]).astype(jnp.float32)
    return jnp.sum(prob_all * picked, axis=-1), prob_all, picked


def solution(mesh):
    n_ep = mesh.shape['ep']
    tok_spec = P(('dp', 'ep'), None)
    row_spec = P(('dp', 'ep'))
    exp_spec = P('ep', None, None)

    def local_step(tok_x, tok_dy, exp_first, exp_second, eligible, slot_first, slot_second,
                   ln_weight, ln_bias, router, w_gate, w_up, w_down):
        n_local, d_model = tok_x.shape
        n_exp = eligible.shape[1]
        local_exp = w_gate.shape[0]
        slot_cap = 3 * n_local // n_exp
        f32 = jnp.float32
        hidden, x_hat, inv_std = layer_norm(tok_x, ln_weight, ln_bias)
        logits = jnp.dot(hidden, router, preferred_element_type=f32)
        expert_ids = jnp.arange(n_exp)
        allowed = eligible > 0
        gate_one, prob_one, pick_one = masked_gate(logits, allowed, exp_first)
        gate_two, prob_two, pick_two = masked_gate(logits, allowed & (expert_ids[None, :] != exp_first[:, None]), exp_second)
        row_ids = jnp.arange(n_exp * slot_cap)
        pos_one = jnp.where(slot_first >= 0, exp_first * slot_cap + slot_first, -1)
        pos_two = jnp.where(slot_second >= 0, exp_second * slot_cap + slot_second, -1)
        sel_one = (pos_one[:, None] == row_ids[None, :]).astype(jnp.bfloat16)
        sel_two = (pos_two[:, None] == row_ids[None, :]).astype(jnp.bfloat16)
        sel_both = sel_one + sel_two
        hid_buf = jnp.einsum('tp,td->pd', sel_both, hidden, preferred_element_type=f32).astype(jnp.bfloat16)
        hid_recv = lax.all_to_all(hid_buf.reshape(n_ep, local_exp, slot_cap, d_model), 'ep', 0, 0, tiled=True)
        pre_gate = jnp.einsum('sgcd,gdf->sgcf', hid_recv, w_gate, preferred_element_type=f32)
        pre_up = jnp.einsum('sgcd,gdf->sgcf', hid_recv, w_up, preferred_element_type=f32)
        sig_gate = jax.nn.sigmoid(pre_gate)
        silu_gate = pre_gate * sig_gate
        inner_act = (silu_gate * pre_up).astype(jnp.bfloat16)
        exp_out = jnp.einsum('sgcf,gfd->sgcd', inner_act, w_down, preferred_element_type=f32).astype(jnp.bfloat16)
        out_back = lax.all_to_all(exp_out, 'ep', 0, 0, tiled=True).reshape(n_exp * slot_cap, d_model)
        out_one = jnp.dot(sel_one, out_back, preferred_element_type=f32)
        out_two = jnp.dot(sel_two, out_back, preferred_element_type=f32)
        y_mix = gate_one[:, None] * out_one + gate_two[:, None] * out_two
        out_tok = (tok_x.astype(f32) + y_mix).astype(jnp.bfloat16)
        dy_float = tok_dy.astype(f32)
        grad_one = (gate_one[:, None] * dy_float).astype(jnp.bfloat16)
        grad_two = (gate_two[:, None] * dy_float).astype(jnp.bfloat16)
        grad_buf = (jnp.einsum('tp,td->pd', sel_one, grad_one, preferred_element_type=f32)
                    + jnp.einsum('tp,td->pd', sel_two, grad_two, preferred_element_type=f32)).astype(jnp.bfloat16)
        grad_recv = lax.all_to_all(grad_buf.reshape(n_ep, local_exp, slot_cap, d_model), 'ep', 0, 0, tiled=True)
        grad_inner = jnp.einsum('sgcd,gfd->sgcf', grad_recv, w_down, preferred_element_type=f32)
        dw_down = jnp.einsum('sgcf,sgcd->gfd', inner_act, grad_recv, preferred_element_type=f32)
        grad_pre_gate = (grad_inner * pre_up * sig_gate * (1.0 + pre_gate * (1.0 - sig_gate))).astype(jnp.bfloat16)
        grad_pre_up = (grad_inner * silu_gate).astype(jnp.bfloat16)
        dw_gate = jnp.einsum('sgcd,sgcf->gdf', hid_recv, grad_pre_gate, preferred_element_type=f32)
        dw_up = jnp.einsum('sgcd,sgcf->gdf', hid_recv, grad_pre_up, preferred_element_type=f32)
        grad_hid = (jnp.einsum('sgcf,gdf->sgcd', grad_pre_gate, w_gate, preferred_element_type=f32)
                    + jnp.einsum('sgcf,gdf->sgcd', grad_pre_up, w_up, preferred_element_type=f32)).astype(jnp.bfloat16)
        hid_back = lax.all_to_all(grad_hid, 'ep', 0, 0, tiled=True).reshape(n_exp * slot_cap, d_model)
        grad_exp = jnp.dot(sel_both, hid_back, preferred_element_type=f32)
        dgate_one = jnp.sum(dy_float * out_one, axis=-1)
        dgate_two = jnp.sum(dy_float * out_two, axis=-1)
        d_logits = ((dgate_one * gate_one)[:, None] * (pick_one - prob_one)
                    + (dgate_two * gate_two)[:, None] * (pick_two - prob_two)).astype(jnp.bfloat16)
        d_router = jnp.einsum('td,te->de', hidden, d_logits, preferred_element_type=f32)
        grad_h = jnp.einsum('te,de->td', d_logits, router, preferred_element_type=f32) + grad_exp
        d_ln_weight = jnp.sum(grad_h * x_hat, axis=0)
        d_ln_bias = jnp.sum(grad_h, axis=0)
        dx_tok = (dy_float + layer_norm_back(grad_h, x_hat, inv_std, ln_weight)).astype(jnp.bfloat16)
        dw_gate = lax.psum(dw_gate, 'dp')
        dw_up = lax.psum(dw_up, 'dp')
        dw_down = lax.psum(dw_down, 'dp')
        d_router = lax.psum(d_router, ('dp', 'ep'))
        d_ln_weight = lax.psum(d_ln_weight, ('dp', 'ep'))
        d_ln_bias = lax.psum(d_ln_bias, ('dp', 'ep'))
        return out_tok, dx_tok, dw_gate, dw_up, dw_down, d_router, d_ln_weight, d_ln_bias

    return jax.shard_map(
        local_step, mesh=mesh,
        in_specs=(tok_spec, tok_spec, row_spec, row_spec, tok_spec, row_spec, row_spec,
                  P(), P(), P(), exp_spec, exp_spec, exp_spec),
        out_specs=(tok_spec, tok_spec, exp_spec, exp_spec, exp_spec, P(), P(), P()),
        check_vma=False)
```

profile of v0, /device:TPU:0, one launch (start us, length us, event | category | flops | bytes accessed | tf_op | source)
XLA Modules:
  0.0 5319.2 jit_solution(10941216292663288485)
XLA Ops:
  7.2 0.9 convert_element_type.73
  8.0 1.2 convert_element_type.72
  9.2 4.7 convert_reduce_fusion
  14.0 5.7 fusion.29
  19.7 4.6 fusion.24
  24.4 33.4 convolution_convert_fusion
  57.8 9.0 all-to-all-start
  66.8 5.7 fusion.78
  72.6 0.1 select_reduce_fusion.1
  72.7 0.4 copy-done.2
  73.2 0.0 copy-done.26
  73.2 34.2 fusion.49
  107.5 38.2 add_convert_fusion.1
  145.7 194.7 %all-to-all-done = bf16[4,4,192,4096]{3,2,1,0:T(8,128)(2,1)} async-done(((bf16[4,4,192,4096]{3,2,1,0:T(8,128)(2,1)}), bf16[4,4,192,4096]{3,2,1,0:T(8,128)(2,1)}, u32[]{:S(2)}, u32[]{:S(2)}) %all-to-all-start) | async-done | bytes 25165856 | tf_op jit(solution)/shard_map/all_to_all | solution.py:57
  340.4 8.4 all-to-all-start.2
  348.8 0.0 all-reduce.8.cloned.1.call-start
  348.9 33.7 fusion.2
  382.6 33.5 fusion.6
  416.1 205.4 %all-to-all-done.2 = bf16[4,4,192,4096]{3,2,1,0:T(8,128)(2,1)} async-done(((bf16[4,4,192,4096]{3,2,1,0:T(8,128)(2,1)}), bf16[4,4,192,4096]{3,2,1,0:T(8,128)(2,1)}, u32[]{:S(2)}, u32[]{:S(2)}) %all-to-all-start.2) | async-done | bytes 25165856 | tf_op jit(solution)/shard_map/all_to_all | solution.py:74
  621.4 46.4 fusion.40
  667.9 34.5 convert_bitcast_fusion
  702.3 12.2 copy.29
  714.6 278.1 %all_to_all.20 = bf16[4,4,192,4096]{3,2,1,0:T(8,128)(2,1)} all-to-all(bf16[4,4,192,4096]{3,2,1,0:T(8,128)(2,1)S(1)} %copy.29), channel_id=1, replica_groups=mesh['dp'=2,'ep'=4] {'ep'}, dimensions={0} | all-to-all | bytes 50331648 | tf_op jit(solution)/shard_map/all_to_all | solution.py:64
  992.7 31.6 fusion.47
  1024.4 36.7 fusion.31
  1061.2 0.6 copy-done.29
  1061.7 0.6 copy-done.31
  1062.4 5.3 fusion.80
  1067.7 0.0 all-reduce.8.cloned.1.call-update
  1067.7 0.0 all-reduce.6.cloned.1.call-start
  1067.8 39.5 convolution_bitcast_fusion
  1107.3 0.0 all-reduce.10.cloned.1.call-start
  1107.3 38.6 convolution_bitcast_fusion.2
  1145.9 38.9 convolution_bitcast_fusion.1
  1184.8 37.7 fusion
  1222.5 42.8 fusion.12
  1265.3 12.2 copy.31
  1277.6 278.1 %all_to_all.21 = bf16[4,4,192,4096]{3,2,1,0:T(8,128)(2,1)} all-to-all(bf16[4,4,192,4096]{3,2,1,0:T(8,128)(2,1)S(1)} %copy.31), channel_id=1, replica_groups=mesh['dp'=2,'ep'=4] {'ep'}, dimensions={0} | all-to-all | bytes 50331648 | tf_op jit(solution)/shard_map/all_to_all | solution.py:83
  1555.8 31.8 fusion.59
  1587.8 15.2 fusion.28
  1602.9 24.5 all-reduce
  1627.4 16.4 fusion.35
  1643.8 832.3 %all-reduce.6.cloned.1.call-done = f32[4,960,4096]{2,1,0:T(8,128)} async-done(((f32[4,960,4096]{2,1,0:T(8,128)}), f32[4,960,4096]{2,1,0:T(8,128)}) %all-reduce.6.cloned.1.call-update) | async-done | bytes 62914576 | tf_op jit(solution)/shard_map/psum | solution.py:96
  2476.1 2712.4 %all-reduce.10.cloned.1.call-done = (f32[4,4096,960]{1,2,0:T(8,128)}, f32[4,4096,960]{1,2,0:T(8,128)}) async-done(((f32[4,4096,960]{1,2,0:T(8,128)}, f32[4,4096,960]{1,2,0:T(8,128)}), (f32[4,4096,960]{1,2,0:T(8,128)}, f32[4,4096,960]{1,2,0:T(8,128)})) %all-reduce.10.cloned.1.call-update) | async-done | bytes 125829136 | tf_op jit(solution)/shard_map/psum | solution.py:94
  5188.5 40.8 copy.61
  5229.4 41.6 copy.62
  5270.9 40.9 copy.63
  5311.8 0.7 copy.64
  (118 shorter events, 0.4 us)
Async XLA Ops:
  7.2 59.6 %copy-start = (bf16[4096,16]{0,1:T(8,128)(2,1)S(1)}, bf16[4096,16]{0,1:T(8,128)(2,1)}, u32[]{:S(2)}) copy-start(bf16[4096,16]{0,1:T(8,128)(2,1)} %param.22) | copy-start | bytes 393220
  7.2 12.5 slice-start
  9.2 15.1 copy-start.18
  9.2 15.1 copy-start.9
  9.2 15.1 copy-start.20
  9.2 15.1 copy-start.42
  9.2 15.1 copy-start.43
  14.0 43.8 copy-start.34
  19.7 38.1 copy-start.36
  24.3 33.4 copy-start.1
  24.4 48.8 copy-start.47
  24.4 83.1 %copy-start.44 = (s32[1024]{0:T(1024)}, s32[1024]{0:T(1024)S(1)}, u32[]{:S(2)}) copy-start(s32[1024]{0:T(1024)S(1)} %get-tuple-element.30) | copy-start | bytes 12292
  57.8 282.6 %all-to-all-start = ((bf16[4,4,192,4096]{3,2,1,0:T(8,128)(2,1)}), bf16[4,4,192,4096]{3,2,1,0:T(8,128)(2,1)}, u32[]{:S(2)}, u32[]{:S(2)}) async-start(bf16[4,4,192,4096]{3,2,1,0:T(8,128)(2,1)} %bitcast.98), calls=%async_computation | async-start | bytes 50331648 | tf_op jit(solution)/shard_map/all_to_all | solution.py:57
  73.2 34.3 copy-start.38
  340.4 281.0 %all-to-all-start.2 = ((bf16[4,4,192,4096]{3,2,1,0:T(8,128)(2,1)}), bf16[4,4,192,4096]{3,2,1,0:T(8,128)(2,1)}, u32[]{:S(2)}, u32[]{:S(2)}) async-start(bf16[4,4,192,4096]{3,2,1,0:T(8,128)(2,1)} %bitcast.99), calls=%async_computation.2 | async-start | bytes 50331648 | tf_op jit(solution)/shard_map/all_to_all | solution.py:74
  348.8 1295.0 %all-reduce.8.cloned.1.call-start = ((), (), s32[]{:S(2)}) async-start(), calls=%async_computation.5 | async-start | bytes 524288 | tf_op jit(solution)/shard_map/psum | solution.py:97
  714.6 278.1 %copy-start.45 = (s32[1024]{0:T(1024)S(1)}, s32[1024]{0:T(1024)}, u32[]{:S(2)}) copy-start(s32[1024]{0:T(1024)} %copy-done.44) | copy-start | bytes 12292
  992.7 31.6 copy-start.39
  992.7 31.6 copy-start.41
  992.7 31.6 copy-start.48
  1024.4 38.0 copy-start.3
  1024.4 38.0 copy-start.6
  1024.4 38.0 copy-start.10
  1024.4 38.0 copy-start.13
  1024.4 38.0 copy-start.16
  1024.4 38.0 copy-start.21
  1024.4 38.0 copy-start.24
  1024.4 38.0 copy-start.27
  1067.7 1408.4 %all-reduce.6.cloned.1.call-start = ((), (), s32[]{:S(2)}) async-start(), calls=%async_computation.4 | async-start | bytes 125829120 | tf_op jit(solution)/shard_map/psum | solution.py:96
  1107.3 4081.2 %all-reduce.10.cloned.1.call-start = ((), (), s32[]{:S(2)}) async-start(), calls=%async_computation.6 | async-start | bytes 251658240 | tf_op jit(solution)/shard_map/psum | solution.py:94
  1277.6 278.1 %copy-start.46 = (s32[1024]{0:T(1024)S(1)}, s32[1024]{0:T(1024)}, u32[]{:S(2)}) copy-start(s32[1024]{0:T(1024)} %copy-done.44) | copy-start | bytes 12292
  1277.6 278.1 %copy-start.49 = (s32[1024]{0:T(1024)S(1)}, s32[1024]{0:T(1024)}, u32[]{:S(2)}) copy-start(s32[1024]{0:T(1024)} %copy-done.47) | copy-start | bytes 12292
  1277.6 310.0 %slice-start.2 = ((s8[8388608]{0:T(1024)(128)(4,1)}), s8[4194304]{0:T(1024)(128)(4,1)S(1)}, s32[]{:S(2)}) async-start(s8[8388608]{0:T(1024)(128)(4,1)} %bitcast.96), calls=%async_computation.9 | async-start | bytes 8388608
  1555.7 31.9 slice-start.3
  1555.7 31.9 copy-start.4
  1555.7 31.9 copy-start.7
  1555.7 31.9 copy-start.11
  1555.7 31.9 copy-start.14
  1555.7 31.9 copy-start.17
  1555.8 31.9 copy-start.19
  1555.8 31.9 copy-start.22
  1555.8 31.9 copy-start.25
  1555.8 31.9 copy-start.28
  1555.8 31.9 copy-start.30
  1555.8 31.9 copy-start.32
  1555.8 31.9 copy-start.35
  1555.8 31.9 copy-start.37
  5270.9 40.9 copy-start.8
  (11 other events, 25.1 us)
Sparse Core Ops, SparseCore 0:
  1067.8 43.3 all-reduce.7
  1114.3 1361.7 all-reduce.5
  2479.2 2709.3 all-reduce.9
where the time goes:
time: 5330 us; the launch traced here: 5320 us
  waiting for transfers between devices  3940 us (74%)
  blocking collectives  581 us (11%)
  matrix products  578 us (11%)
  local copies, waits for them, and re-layouts  150 us (3%)
    psum x1, waiting for transfers between devices, local_step(): dw_gate = lax.psum(dw_gate, 'dp')  2710 us
    psum x1, waiting for transfers between devices, local_step(): dw_down = lax.psum(dw_down, 'dp')  832 us
    all_to_all x1, blocking collectives, local_step(): lax.all_to_all(exp_out, 'ep', 0, 0, tiled=True)  278 us
    all_to_all x1, blocking collectives, local_step(): lax.all_to_all(grad_hid, 'ep', 0, 0, tiled=True)  278 us
    all_to_all x1, waiting for transfers between devices, local_step(): lax.all_to_all(grad_buf.reshape(n_ep, local_exp, slot_cap, d_model), 'ep'...  205 us
    all_to_all x1, waiting for transfers between devices, local_step(): lax.all_to_all(hid_buf.reshape(n_ep, local_exp, slot_cap, d_model), 'ep',...  195 us
    unnamed x112, local copies, waits for them, and re-layouts  126 us
  transfers between devices with their start and end apart: 5, of which 4 were waited for; matrix products, arithmetic and copies ran while one was open for 8% of the time, Pallas kernels for 0%

commit v1 on v0

v1 whole, which is shorter than its diff:
```python
import jax
import jax.numpy as jnp
from jax import lax
from jax.experimental import pallas as pl
from jax.experimental.pallas import tpu as pltpu
from jax.sharding import PartitionSpec as P

LN_EPS = 1e-5
F32, BF16 = jnp.float32, jnp.bfloat16
VMEM_LIMIT = 60 * 1024 * 1024
ROWS, BOTH_COLS = ((1,), (0,)), ((1,), (1,))


def mm(lhs, rhs, dims=ROWS):
    return lax.dot_general(lhs, rhs, (dims, ((), ())), preferred_element_type=F32)


def call(body, grid, in_specs, out_specs, out_shape, operands, flops, scratch=(), aliases=None):
    return pl.pallas_call(
        body, grid=grid, in_specs=in_specs, out_specs=out_specs, out_shape=out_shape, scratch_shapes=list(scratch),
        input_output_aliases=aliases or {},
        compiler_params=pltpu.CompilerParams(vmem_limit_bytes=VMEM_LIMIT,
                                             dimension_semantics=("arbitrary",) * len(grid)),
        cost_estimate=pl.CostEstimate(flops=flops, transcendentals=0, bytes_accessed=flops // 300))(*operands)


def masked_gate(logits, allowed, choice):
    expert_ids = jnp.arange(logits.shape[-1])
    prob_all = jax.nn.softmax(jnp.where(allowed, logits, -1e30), axis=-1)
    picked = (choice[:, None] == expert_ids[None, :]).astype(F32)
    return jnp.sum(prob_all * picked, axis=-1), prob_all, picked


def gather_rows(tokens, tables, gates, n_exp, cap):
    n_src, (n_tok, d_model), tile, step = len(tokens), tokens[0].shape, 512, 256
    n_slot = n_exp * cap
    extra = [] if gates is None else [gates]

    def body(*refs):
        tok_refs, tab_ref = refs[:n_src], refs[n_src]
        out_ref, hot_ref = refs[-2:]

        @pl.when(pl.program_id(0) == 0)
        def _():
            for s in range(n_src):
                ids = lax.broadcasted_iota(jnp.int32, (n_slot, n_tok), 1)
                hot_ref[s] = (ids == tab_ref[:, s:s + 1]).astype(F32).astype(BF16)

        def col(j, carry):
            at = pl.ds(pl.multiple_of(j * step, step), step)
            for s in range(n_src):
                rows = mm(hot_ref[s], tok_refs[s][:, at])
                if extra:
                    rows = rows * refs[n_src + 1][:, s:s + 1]
                out_ref[:, s * cap:(s + 1) * cap, at] = rows.astype(BF16).reshape(n_exp, cap, step)
            return carry

        lax.fori_loop(0, tile // step, col, 0)

    whole = pl.BlockSpec((n_slot, n_src), lambda j: (0, 0))
    return call(body, (d_model // tile,),
                [pl.BlockSpec((n_tok, tile), lambda j: (0, j))] * n_src + [whole] * (1 + len(extra)),
                pl.BlockSpec((n_exp, n_src * cap, tile), lambda j: (0, 0, j)),
                jax.ShapeDtypeStruct((n_exp, n_src * cap, d_model), BF16),
                (*tokens, tables, *extra), 2 * n_src * n_slot * n_tok * d_model,
                [pltpu.VMEM((n_src, n_slot, n_tok), BF16)])


def stack_rows(refs):
    return refs[0][0] if len(refs) == 1 else jnp.concatenate([r[0] for r in refs], axis=0)


def up_pass(h_sets, q_sets, weights, saved=None):
    h_sets, q_sets, saved = list(h_sets or []), list(q_sets or []), list(saved or [])
    n_exp, _, d_model = (h_sets + q_sets)[0].shape
    n_row = sum(v.shape[1] for v in (h_sets or q_sets))
    d_ff, tile = weights[2].shape[1], 2048
    n_h, n_q = len(h_sets), len(q_sets)
    w_in = ([weights[0], weights[1]] if n_h else []) + ([weights[2]] if n_q else [])
    n_out = 3 if n_h else 2

    def body(*refs):
        refs = list(refs)
        take = lambda n: [refs.pop(0) for _ in range(n)]
        h_refs, q_refs, w_refs, saved_refs, outs, accs = take(n_h), take(n_q), take(len(w_in)), take(len(saved)), take(n_out), refs
        k = pl.program_id(1)

        @pl.when(k == 0)
        def _():
            for acc in accs:
                acc[...] = jnp.zeros_like(acc)

        if n_h:
            h = stack_rows(h_refs)
            accs[0][...] += mm(h, w_refs[0][0], BOTH_COLS)
            accs[1][...] += mm(h, w_refs[1][0], BOTH_COLS)
        if n_q:
            accs[-1][...] += mm(stack_rows(q_refs), w_refs[-1][0], BOTH_COLS)

        @pl.when(k == pl.num_programs(1) - 1)
        def _():
            if n_h:
                a, b = accs[0][...], accs[1][...]
                sig = jax.nn.sigmoid(a)
                silu = a * sig
                outs[0][0] = (silu * b).astype(BF16)
                slope = b * sig * (1.0 + a * (1.0 - sig))
            else:
                slope, silu = saved_refs[0][0], saved_refs[1][0]
            if n_q:
                du = accs[-1][...]
                outs[-2][0] = (du * slope).astype(BF16)
                outs[-1][0] = (du * silu).astype(BF16)
            else:
                outs[-2][0] = slope
                outs[-1][0] = silu

    row = lambda v: pl.BlockSpec((1, v.shape[1], tile), lambda e, k: (e, 0, k))
    wide = pl.BlockSpec((1, d_ff, tile), lambda e, k: (e, 0, k))
    act = pl.BlockSpec((1, n_row, d_ff), lambda e, k: (e, 0, 0))
    shape = lambda t: jax.ShapeDtypeStruct((n_exp, n_row, d_ff), t)
    shapes = ([shape(BF16)] if n_h else []) + [shape(BF16 if n_q else F32)] * 2
    return call(body, (n_exp, d_model // tile),
                [row(v) for v in h_sets + q_sets] + [wide] * len(w_in) + [act] * len(saved),
                [act] * n_out, shapes, (*h_sets, *q_sets, *w_in, *saved),
                2 * n_exp * n_row * d_model * d_ff * len(w_in),
                [pltpu.VMEM((n_row, d_ff), F32)] * len(w_in))


def down_pass(inner, d_gate, d_up, weights, cap, picks):
    has_o, has_d = inner is not None, d_gate is not None
    acts = ([inner] if has_o else []) + ([d_gate, d_up] if has_d else [])
    w_in = ([weights[2]] if has_o else []) + ([weights[0], weights[1]] if has_d else [])
    n_exp, _, d_ff = acts[0].shape
    d_model, tile, n_src = weights[2].shape[2], 1024, len(picks)

    def body(*refs):
        refs = list(refs)
        take = lambda n: [refs.pop(0) for _ in range(n)]
        rows = [take(n_src) for _ in acts]
        w_refs = take(len(acts))
        if has_o:
            out = mm(stack_rows(rows[0]), w_refs[0][0]).astype(BF16)
            for s in range(n_src):
                refs.pop(0)[0] = out[s * cap:(s + 1) * cap]
        if has_d:
            back = (mm(stack_rows(rows[-2]), w_refs[-2][0]) + mm(stack_rows(rows[-1]), w_refs[-1][0])).astype(BF16)
            for s in range(n_src):
                refs.pop(0)[0] = back[s * cap:(s + 1) * cap]

    wide = pl.BlockSpec((1, d_ff, tile), lambda e, j: (e, 0, j))
    act = [pl.BlockSpec((1, cap, d_ff), lambda e, j, p=p: (e, p, 0)) for p in picks]
    n_out = n_src * (has_o + has_d)
    return call(body, (n_exp, d_model // tile),
                act * len(acts) + [wide] * len(w_in),
                [pl.BlockSpec((1, cap, tile), lambda e, j: (e, 0, j))] * n_out,
                [jax.ShapeDtypeStruct((n_exp, cap, d_model), BF16)] * n_out,
                (*[a for a in acts for _ in picks], *w_in),
                2 * n_exp * n_src * cap * d_model * d_ff * len(acts))


def weight_grads(h_sets, q_sets, acts, before=None):
    n_exp, _, d_model = h_sets[0].shape
    n_row = sum(v.shape[1] for v in h_sets)
    d_ff, tile = acts[0][0].shape[2], 512
    before = list(before or [])
    n_set, n_grp = len(h_sets), len(acts)

    def body(*refs):
        refs = list(refs)
        take = lambda n: [refs.pop(0) for _ in range(n)]
        h_refs, q_refs, act_refs, prev, outs, act_ref = take(n_set), take(n_set), [take(n_grp) for _ in range(3)], take(len(before)), take(3), refs[0]

        @pl.when(pl.program_id(1) == 0)
        def _():
            for i in range(3):
                at = 0
                for r in act_refs[i]:
                    act_ref[i, :, at:at + r.shape[1]] = r[0].T
                    at += r.shape[1]

        h, q = stack_rows(h_refs), stack_rows(q_refs)
        for i, rows in ((0, q), (1, h), (2, h)):
            total = mm(act_ref[i], rows)
            outs[i][0] = prev[i][0] + total if prev else total

    row = lambda v: pl.BlockSpec((1, v.shape[1], tile), lambda e, i: (e, 0, i))
    act = lambda v: pl.BlockSpec((1, v.shape[1], d_ff), lambda e, i: (e, 0, 0))
    wide = pl.BlockSpec((1, d_ff, tile), lambda e, i: (e, 0, i))
    flat = [grp[i] for i in range(3) for grp in acts]
    return call(body, (n_exp, d_model // tile),
                [row(v) for v in (*h_sets, *q_sets)] + [act(v) for v in flat] + [wide] * len(before), [wide] * 3,
                [jax.ShapeDtypeStruct((n_exp, d_ff, d_model), F32)] * 3,
                (*h_sets, *q_sets, *flat, *before), 6 * n_exp * n_row * d_model * d_ff,
                [pltpu.VMEM((3, d_ff, n_row), BF16)],
                {2 * n_set + 3 * n_grp + i: i for i in range(3)} if before else None)


def one_hot(pos, n_slot):
    return (lax.broadcasted_iota(jnp.int32, (pos.shape[0], n_slot), 1) == pos).astype(F32).astype(BF16)


def combine_out(blocks, pos, gates, base, tok_dy, dg_base=None):
    n_blk = len(blocks)
    n_exp, cap, d_model = blocks[0].shape
    n_tok, tile, step = tok_dy.shape[0], 512, 256
    n_slot = n_exp * cap
    extra = [] if dg_base is None else [dg_base]

    def body(*refs):
        blk = refs[:n_blk]
        pos_ref, gate_ref, base_ref, dy_ref = refs[n_blk:n_blk + 4]
        out_ref, dg_ref, hot_one, hot_two = refs[-4:]

        @pl.when(pl.program_id(0) == 0)
        def _():
            dg_ref[...] = refs[n_blk + 4][...] if extra else jnp.zeros_like(dg_ref)
            for f in range(n_blk):
                hot_one[f] = one_hot(pos_ref[:, f:f + 1], n_slot)
                hot_two[f] = one_hot(pos_ref[:, n_blk + f:n_blk + f + 1], n_slot)

        def col(j, carry):
            at = pl.ds(pl.multiple_of(j * step, step), step)
            o_one = sum(mm(hot_one[f], blk[f][:, :, at].reshape(n_slot, step)) for f in range(n_blk))
            o_two = sum(mm(hot_two[f], blk[f][:, :, at].reshape(n_slot, step)) for f in range(n_blk))
            dy = dy_ref[:, at].astype(F32)
            mix = gate_ref[:, 0:1] * o_one + gate_ref[:, 1:2] * o_two
            out_ref[:, at] = (base_ref[:, at].astype(F32) + mix).astype(out_ref.dtype)
            dg_ref[:, 0:1] += jnp.sum(dy * o_one, axis=1, keepdims=True)
            dg_ref[:, 1:2] += jnp.sum(dy * o_two, axis=1, keepdims=True)
            return carry

        lax.fori_loop(0, tile // step, col, 0)

    tok = pl.BlockSpec((n_tok, tile), lambda j: (0, j))
    small = lambda n: pl.BlockSpec((n_tok, n), lambda j: (0, 0))
    return call(body, (d_model // tile,),
                [pl.BlockSpec((n_exp, cap, tile), lambda j: (0, 0, j))] * n_blk + [small(2 * n_blk), small(2), tok, tok]
                + [small(2)] * len(extra), [tok, small(2)],
                [jax.ShapeDtypeStruct((n_tok, d_model), BF16 if extra else F32), jax.ShapeDtypeStruct((n_tok, 2), F32)],
                (*blocks, pos, gates, base, tok_dy, *extra), 4 * n_tok * n_blk * n_slot * d_model,
                [pltpu.VMEM((n_blk, n_tok, n_slot), BF16)] * 2)


def pair_hot(hot_ref, pos_ref, n_blk, n_slot):
    for f in range(n_blk):
        hot_ref[f] = (one_hot(pos_ref[:, f:f + 1], n_slot)
                      + one_hot(pos_ref[:, n_blk + f:n_blk + f + 1], n_slot))


def combine_part(blocks, pos):
    n_blk = len(blocks)
    n_exp, cap, d_model = blocks[0].shape
    n_tok, tile, step = pos.shape[0], 512, 256
    n_slot = n_exp * cap

    def body(*refs):
        blk, (pos_ref, out_ref, hot_ref) = refs[:n_blk], refs[n_blk:]

        @pl.when(pl.program_id(0) == 0)
        def _():
            pair_hot(hot_ref, pos_ref, n_blk, n_slot)

        def col(j, carry):
            at = pl.ds(pl.multiple_of(j * step, step), step)
            out_ref[:, at] = sum(mm(hot_ref[f], blk[f][:, :, at].reshape(n_slot, step)) for f in range(n_blk))
            return carry

        lax.fori_loop(0, tile // step, col, 0)

    return call(body, (d_model // tile,),
                [pl.BlockSpec((n_exp, cap, tile), lambda j: (0, 0, j))] * n_blk + [pl.BlockSpec((n_tok, 2 * n_blk), lambda j: (0, 0))],
                pl.BlockSpec((n_tok, tile), lambda j: (0, j)), jax.ShapeDtypeStruct((n_tok, d_model), F32),
                (*blocks, pos), 2 * n_tok * n_blk * n_slot * d_model, [pltpu.VMEM((n_blk, n_tok, n_slot), BF16)])


def combine_back(blocks, pos, part, tok_x, tok_dy, stats, d_logits, router, ln_weight):
    n_blk = len(blocks)
    n_exp, cap, d_model = blocks[0].shape
    n_tok, tile, step = tok_x.shape[0], 512, 256
    n_slot, n_tile = n_exp * cap, d_model // 512

    def body(*refs):
        blk = refs[:n_blk]
        (pos_ref, part_ref, x_ref, dy_ref, stat_ref, dl_ref, rt_ref, lnw_ref,
         dx_ref, dw_ref, db_ref, hot_ref, gh_ref, m1_ref, m2_ref) = refs[n_blk:]
        phase, j = pl.program_id(0), pl.program_id(1)

        @pl.when((phase == 0) & (j == 0))
        def _():
            m1_ref[...] = jnp.zeros_like(m1_ref)
            m2_ref[...] = jnp.zeros_like(m2_ref)
            pair_hot(hot_ref, pos_ref, n_blk, n_slot)

        @pl.when(phase == 0)
        def _():
            def col(i, carry):
                at = pl.ds(pl.multiple_of(i * step, step), step)
                grad = sum(mm(hot_ref[f], blk[f][:, :, at].reshape(n_slot, step)) for f in range(n_blk))
                grad = mm(dl_ref[...], rt_ref[:, at]) + (part_ref[:, at] + grad)
                gh_ref[j, :, at] = grad
                x_hat = (x_ref[:, at].astype(F32) - stat_ref[:, 0:1]) * stat_ref[:, 1:2]
                scaled = grad * lnw_ref[:, at].astype(F32)
                m1_ref[...] += jnp.sum(scaled, axis=1, keepdims=True)
                m2_ref[...] += jnp.sum(scaled * x_hat, axis=1, keepdims=True)
                dw_ref[:, at] = jnp.sum(grad * x_hat, axis=0, keepdims=True)
                db_ref[:, at] = jnp.sum(grad, axis=0, keepdims=True)
                return carry

            lax.fori_loop(0, tile // step, col, 0)

        @pl.when(phase == 1)
        def _():
            x_hat = (x_ref[...].astype(F32) - stat_ref[:, 0:1]) * stat_ref[:, 1:2]
            scaled = gh_ref[j] * lnw_ref[...].astype(F32)
            d_ln = stat_ref[:, 1:2] * (scaled - m1_ref[...] / d_model - x_hat * (m2_ref[...] / d_model))
            dx_ref[...] = (dy_ref[...].astype(F32) + d_ln).astype(BF16)

    last = n_tile - 1
    early = lambda p, j: j * (1 - p) + last * p
    tok = pl.BlockSpec((n_tok, tile), lambda p, j: (0, j))
    tok_early = pl.BlockSpec((n_tok, tile), lambda p, j: (0, early(p, j)))
    tok_late = pl.BlockSpec((n_tok, tile), lambda p, j: (0, j * p))
    wide = lambda n: pl.BlockSpec((n, tile), lambda p, j: (0, j))
    wide_early = lambda n: pl.BlockSpec((n, tile), lambda p, j: (0, early(p, j)))
    small = lambda n: pl.BlockSpec((n_tok, n), lambda p, j: (0, 0))
    return call(body, (2, n_tile),
                [pl.BlockSpec((n_exp, cap, tile), lambda p, j: (0, 0, early(p, j)))] * n_blk
                + [small(2 * n_blk), tok_early, tok, tok_late, small(2), small(router.shape[0]), wide(router.shape[0]), wide(1)],
                [tok_late, wide_early(1), wide_early(1)],
                [jax.ShapeDtypeStruct((n_tok, d_model), BF16)] + [jax.ShapeDtypeStruct((1, d_model), F32)] * 2,
                (*blocks, pos, part, tok_x, tok_dy, stats, d_logits, router, ln_weight), 2 * n_tok * n_blk * n_slot * d_model,
                [pltpu.VMEM((n_blk, n_tok, n_slot), BF16), pltpu.VMEM((n_tile, n_tok, tile), F32)]
                + [pltpu.VMEM((n_tok, 1), F32)] * 2)


def solution(mesh):
    n_dp, n_ep = mesh.shape['dp'], mesh.shape['ep']
    tok_spec = P(('dp', 'ep'), None)
    row_spec = P(('dp', 'ep'))
    exp_spec = P('ep', None, None)

    def swap(value, flip_dp, flip_ep):
        pairs = [(d * n_ep + e, (d ^ flip_dp) * n_ep + (e ^ flip_ep)) for d in range(n_dp) for e in range(n_ep)]
        return lax.ppermute(value, ('dp', 'ep'), pairs)

    def local_step(tok_x, tok_dy, exp_first, exp_second, eligible, slot_first, slot_second,
                   ln_weight, ln_bias, router, w_gate, w_up, w_down):
        n_local, _ = tok_x.shape
        n_exp = eligible.shape[1]
        local_exp = w_gate.shape[0]
        cap = 3 * n_local // n_exp
        n_slot = local_exp * cap
        me = lax.axis_index('ep')
        weights = (jnp.swapaxes(w_gate, 1, 2), jnp.swapaxes(w_up, 1, 2), w_down)

        x_float = tok_x.astype(F32)
        mean = jnp.mean(x_float, axis=-1, keepdims=True)
        centered = x_float - mean
        inv_std = lax.rsqrt(jnp.mean(centered * centered, axis=-1, keepdims=True) + LN_EPS)
        hidden = (centered * inv_std * ln_weight.astype(F32) + ln_bias.astype(F32)).astype(BF16)
        logits = jnp.dot(hidden, router, preferred_element_type=F32)
        expert_ids = jnp.arange(n_exp)
        allowed = eligible > 0
        gate_one, prob_one, pick_one = masked_gate(logits, allowed, exp_first)
        gate_two, prob_two, pick_two = masked_gate(logits, allowed & (expert_ids[None, :] != exp_first[:, None]), exp_second)
        pos_one = jnp.where(slot_first >= 0, exp_first * cap + slot_first, -1)
        pos_two = jnp.where(slot_second >= 0, exp_second * cap + slot_second, -1)
        row_ids = jnp.arange(n_exp * cap)
        hit_one = pos_one[:, None] == row_ids[None, :]
        hit_two = pos_two[:, None] == row_ids[None, :]
        slot_tok = jnp.max(jnp.where(hit_one | hit_two, jnp.arange(n_local)[:, None], -1), axis=0).astype(F32)
        slot_gate = jnp.sum(jnp.where(hit_one, gate_one[:, None], 0.0) + jnp.where(hit_two, gate_two[:, None], 0.0), axis=0)
        meta = jnp.stack([slot_tok, slot_gate])

        def columns(*tables):
            mine = [lax.dynamic_slice(t, (0, me * n_slot), (2, n_slot)) for t in tables]
            both = jnp.stack(mine, axis=-1)
            return both[0].astype(jnp.int32), both[1]

        def spread(value):
            from_x = swap(value, 0, 2)
            from_y = swap(value, 1, 0)
            from_d = swap(from_x, 1, 0)
            return [(v, swap(v, 0, 1)) for v in
                    (value, from_x, from_y, from_d)]

        (m_a, m_x, m_y, m_d) = spread(meta)
        (h_a, h_x, h_y, h_d) = spread(hidden)
        (g_a, g_x, g_y, g_d) = spread(tok_dy)

        def gath(toks, tables, gated):
            tab, gts = columns(*tables)
            return gather_rows(toks, tab, gts if gated else None, local_exp, cap)

        ha, qa = [gath(h_a, m_a, False)], [gath(g_a, m_a, True)]
        act_a = up_pass(ha, qa, weights)
        o_a0, o_a1, b_a0, b_a1 = down_pass(*act_a, weights, cap, (0, 1))
        m_p, m_r = (m_x[0], m_y[0]), (m_x[1], m_y[1])
        hxy = [gath((h_x[0], h_y[0]), m_p, False), gath((h_x[1], h_y[1]), m_r, False)]
        u_xy, *slopes = up_pass(hxy, None, weights)
        o_x0, o_x1 = down_pass(u_xy, None, None, weights, cap, (0, 2))
        qxy = [gath((g_x[0], g_y[0]), m_p, True), gath((g_x[1], g_y[1]), m_r, True)]
        d_xy = up_pass(None, qxy, weights, slopes)
        b_x0, b_x1 = down_pass(None, *d_xy, weights, cap, (0, 2))
        part = weight_grads(hxy, qxy, [(u_xy, *d_xy)])
        hd = [gath(h_d[i:i + 1], m_d[i:i + 1], False) for i in range(2)]
        u_d, *slopes = up_pass(hd, None, weights)
        qd = [gath(g_d[i:i + 1], m_d[i:i + 1], True) for i in range(2)]
        d_d = up_pass(None, qd, weights, slopes)
        dw_down, dw_gate, dw_up = weight_grads(ha + hd, qa + qd, [act_a, (u_d, *d_d)], part)

        outs = [o_a0, swap(o_a1, 0, 1), swap(o_x0, 0, 2), swap(o_x1, 0, 3)]
        backs = [b_a0, swap(b_a1, 0, 1), swap(b_x0, 0, 2), swap(b_x1, 0, 3)]

        def slots(flips):
            cols = [(p, p - (me ^ f) * n_slot) for p in (pos_one, pos_two) for f in flips]
            return jnp.stack([jnp.where(p < 0, -1, at) for p, at in cols], axis=-1)

        near, far = slots((0, 1)), slots((2, 3))
        gates = jnp.stack([gate_one, gate_two], axis=-1)
        mix, dgate = combine_out(outs[:2], near, gates, tok_x, tok_dy)
        out_tok, dgate = combine_out(outs[2:], far, gates, mix, tok_dy, dgate)
        d_logits = ((dgate[:, 0] * gate_one)[:, None] * (pick_one - prob_one)
                    + (dgate[:, 1] * gate_two)[:, None] * (pick_two - prob_two)).astype(BF16)
        d_router = jnp.einsum('te,td->ed', d_logits, hidden, preferred_element_type=F32)

        def sum_all(value):
            for flips in ((0, 1), (1, 0), (0, 2)):
                value = value + swap(value, *flips)
            return value

        d_router = sum_all(d_router)
        part_back = combine_part(backs[:2], near)
        dx_tok, d_lnw, d_lnb = combine_back(backs[2:], far, part_back, tok_x, tok_dy,
                                            jnp.concatenate([mean, inv_std], axis=1), d_logits, router.T, ln_weight[None, :])
        d_ln = sum_all(jnp.concatenate([d_lnw, d_lnb], axis=0))
        return (out_tok, dx_tok, jnp.swapaxes(dw_gate, 1, 2), jnp.swapaxes(dw_up, 1, 2), dw_down, d_router.T, d_ln[0], d_ln[1])

    return jax.shard_map(
        local_step, mesh=mesh,
        in_specs=(tok_spec, tok_spec, row_spec, row_spec, tok_spec, row_spec, row_spec,
                  P(), P(), P(), exp_spec, exp_spec, exp_spec),
        out_specs=(tok_spec, tok_spec, exp_spec, exp_spec, exp_spec, P(), P(), P()),
        check_vma=False)
```

time: 5330 us -> 1640 us (0.31)
  waiting for transfers between devices: 3940 us -> 631 us
  Pallas kernels: 0 us -> 916 us
  blocking collectives: 581 us -> 0 us
  matrix products: 578 us -> 10.4 us
  local copies, waits for them, and re-layouts: 150 us -> 14.5 us
    psum x3 -> x0, waiting for transfers between devices: 3540 us -> none  [the longest x1 2710 us: local_step(): dw_gate = lax.psum(dw_gate, 'dp')]
    pallas_call x0 -> x24, Pallas kernels: none -> 916 us  [call(): pl.pallas_call(body, grid=grid, in_specs=in_specs, out_specs=out_specs, o...]
    ppermute x0 -> x33, waiting for transfers between devices: none -> 631 us  [swap(): return lax.ppermute(value, ('dp', 'ep'), pairs)]
    dot_general x18 -> x2, matrix products: 578 us -> 10.4 us  [the longest x1 5.76 us: local_step(): logits = jnp.dot(hidden, router, preferred_element_type=F32)]
    all_to_all x2 -> x0, blocking collectives: 556 us -> none  [the longest x1 278 us: local_step(): lax.all_to_all(exp_out, 'ep', 0, 0, tiled=True)]
    all_to_all x2 -> x0, waiting for transfers between devices: 400 us -> none  [the longest x1 205 us: local_step(): lax.all_to_all(grad_buf.reshape(n_ep, local_exp, slot_cap, d_model), 'ep'...]
    unnamed x112 -> x51, local copies, waits for them, and re-layouts: 126 us -> 1.36 us
  transfers between devices with their start and end apart: 5 -> 33, of which waited for: 4 -> 7; matrix products, arithmetic and copies ran while one was open for 8% -> 3% of each run, Pallas kernels for 0% -> 44%
where the time goes in v1:
time: 1640 us; the launch traced here: 1630 us
  Pallas kernels  916 us (56%)
  waiting for transfers between devices  631 us (38%)
  other arithmetic  35.5 us (2%)
  starting transfers between devices  25.5 us (2%)
    pallas_call x24, Pallas kernels, call(): pl.pallas_call(body, grid=grid, in_specs=in_specs, out_specs=out_specs, o...  916 us
    ppermute x33, waiting for transfers between devices, swap(): return lax.ppermute(value, ('dp', 'ep'), pairs)  631 us
  transfers between devices with their start and end apart: 33, of which 7 were waited for; matrix products, arithmetic and copies ran while one was open for 3% of the time, Pallas kernels for 44%

profile of v1, /device:TPU:0, one launch (start us, length us, event | category | flops | bytes accessed | tf_op | source)
XLA Modules:
  0.0 1634.8 jit_solution(13630914555367103380)
XLA Ops:
  0.7 4.7 convert_reduce_fusion
  6.4 2.3 fusion.2
  8.8 6.7 fusion.5.refs_0_
  16.4 3.8 select_reduce_fusion
  20.4 5.8 fusion.25
  28.0 1.7 select_reduce_fusion.1
  29.7 5.3 add_reduce_fusion
  35.5 2.5 collective-permute-start.3
  38.0 1.5 collective-permute-start.2
  39.9 1.5 collective-permute-done.11
  41.4 2.9 collective-permute-start.1
  47.3 19.9 %shard_map.192.refs_0_ = bf16[4,384,4096]{2,1,0:T(8,128)(2,1)} custom-call(bf16[1024,4096]{1,0:T(8,128)(2,1)} %fusion.5.refs_0_, bf16[1024,4096]{1,0:T(8,128)(2,1)} %collective-permute-done.10.refs_1_, s32[768,2]{1,0:T(8,128)} %get-tuple-element.95.refs_2_), custom_call_target="tpu_custom_call" | custom-call | flops 12884901888 | bytes 42949672 | tf_op jit(solution)/shard_map/pallas_call | solution.py:19
  67.8 20.1 %shard_map.193.refs_1_.refs_3_ = bf16[4,384,4096]{2,1,0:T(8,128)(2,1)} custom-call(bf16[1024,4096]{1,0:T(8,128)(2,1)} %refs_5_.5, bf16[1024,4096]{1,0:T(8,128)(2,1)} %collective-permute-done.12.refs_1_, s32[768,2]{1,0:T(8,128)} %get-tuple-element.95.refs_2_, f32[768,2]{1,0:T(8,128)} %get-tuple-element.94.refs_3_), custom_call_target="tpu_custom_call" | custom-call | flops 12884901888 | bytes 42949672 | tf_op jit(solution)/shard_map/pallas_call | solution.py:19
  88.3 54.9 %shard_map.194 = (bf16[4,384,960]{2,1,0:T(8,128)(2,1)}, bf16[4,384,960]{2,1,0:T(8,128)(2,1)}, bf16[4,384,960]{2,1,0:T(8,128)(2,1)}) custom-call(bf16[4,384,4096]{2,1,0:T(8,128)(2,1)} %shard_map.192.refs_0_, bf16[4,384,4096]{2,1,0:T(8,128)(2,1)} %shard_map.193.refs_1_.refs_3_, bf16[4,960,4096]{2,1,0:T(8,128)(2,1)} %bitcast.79, ...), custom_call_target="tpu_custom_call" | custom-call | flops 36238786560 | bytes 120795952 | tf_op jit(solution)/shard_map/pallas_call | solution.py:19
  143.2 82.6 %collective-permute-done.22 = f32[2,3072]{1,0:T(2,128)S(1)} collective-permute-done((f32[2,3072]{1,0:T(2,128)S(1)}, f32[2,3072]{1,0:T(2,128)S(1)}, u32[]{:S(2)}, u32[]{:S(2)}) %collective-permute-start.22) | collective-permute-done | bytes 24608 | tf_op jit(solution)/shard_map/ppermute | solution.py:345
  225.8 1.7 collective-permute-start.15
  227.6 52.5 %shard_map.195 = (bf16[4,192,4096]{2,1,0:T(8,128)(2,1)}, bf16[4,192,4096]{2,1,0:T(8,128)(2,1)}, bf16[4,192,4096]{2,1,0:T(8,128)(2,1)}, bf16[4,192,4096]{2,1,0:T(8,128)(2,1)}) custom-call(bf16[4,384,960]{2,1,0:T(8,128)(2,1)} %get-tuple-element.45.refs_0_.refs_1_.refs_6_, bf16[4,384,960]{2,1,0:T(8,128)(2,1)} %get-tuple-element.45.refs_0_.refs_1_.refs_6_, ...), custom_call_target="tpu_custom_call" | custom-call | flops 36238786560 | bytes 120795952 | tf_op jit(solution)/shard_map/pallas_call | solution.py:19
  281.1 127.0 %collective-permute-done.14.refs_0_ = bf16[1024,4096]{1,0:T(8,128)(2,1)} collective-permute-done((bf16[1024,4096]{1,0:T(8,128)(2,1)}, bf16[1024,4096]{1,0:T(8,128)(2,1)}, u32[]{:S(2)}, u32[]{:S(2)}) %collective-permute-start.14) | collective-permute-done | bytes 8388640 | tf_op jit(solution)/shard_map/ppermute | solution.py:345
  422.7 20.0 %shard_map.188.refs_0_ = bf16[4,384,4096]{2,1,0:T(8,128)(2,1)} custom-call(bf16[1024,4096]{1,0:T(8,128)(2,1)} %collective-permute-done.refs_0_, bf16[1024,4096]{1,0:T(8,128)(2,1)} %collective-permute-done.1.refs_1_, s32[768,2]{1,0:T(8,128)} %get-tuple-element.93.refs_2_), custom_call_target="tpu_custom_call" | custom-call | flops 12884901888 | bytes 42949672 | tf_op jit(solution)/shard_map/pallas_call | solution.py:19
  443.2 20.1 %shard_map.198.refs_0_.refs_2_ = bf16[4,384,4096]{2,1,0:T(8,128)(2,1)} custom-call(bf16[1024,4096]{1,0:T(8,128)(2,1)} %collective-permute-done.14.refs_0_, bf16[1024,4096]{1,0:T(8,128)(2,1)} %collective-permute-done.15.refs_1_, s32[768,2]{1,0:T(8,128)} %get-tuple-element.93.refs_2_, f32[768,2]{1,0:T(8,128)} %get-tuple-element.92.refs_3_), custom_call_target="tpu_custom_call" | custom-call | flops 12884901888 | bytes 42949672 | tf_op jit(solution)/shard_map/pallas_call | solution.py:19
  463.2 21.3 %shard_map.202.refs_3_ = f32[1024,4096]{1,0:T(8,128)} custom-call(bf16[4,192,4096]{2,1,0:T(8,128)(2,1)} %get-tuple-element.59.refs_0_, bf16[4,192,4096]{2,1,0:T(8,128)(2,1)} %collective-permute-done.20.refs_1_, s32[1024,4]{1,0:T(8,128)} %copy.95.refs_2_), custom_call_target="tpu_custom_call" | custom-call | flops 12884901888 | bytes 42949672 | tf_op jit(solution)/shard_map/pallas_call | solution.py:19
  484.8 38.4 %shard_map.196 = (f32[1024,4096]{1,0:T(8,128)}, f32[1024,2]{1,0:T(8,128)}) custom-call(bf16[4,192,4096]{2,1,0:T(8,128)(2,1)} %get-tuple-element.48.refs_0_, bf16[4,192,4096]{2,1,0:T(8,128)(2,1)} %collective-permute-done.13.refs_1_, s32[1024,4]{1,0:T(8,128)} %copy.95.refs_2_, f32[1024,2]{1,0:T(8,128)} %copy.98.refs_3_, bf16[1024,4096]{1,0:T(8,128)(2,1)} %refs_4_.5, ...), custom_call_target="tpu_custom_call" | custom-call | flops 25769803776 | bytes 85899344 | tf_op jit(solution)/shard_map/pallas_call | solution.py:19
  523.1 1.8 collective-permute-start.25
  524.9 19.9 %shard_map.189.refs_1_ = bf16[4,384,4096]{2,1,0:T(8,128)(2,1)} custom-call(bf16[1024,4096]{1,0:T(8,128)(2,1)} %collective-permute-done.4.refs_0_, bf16[1024,4096]{1,0:T(8,128)(2,1)} %collective-permute-done.5.refs_1_, s32[768,2]{1,0:T(8,128)} %get-tuple-element.91.refs_2_), custom_call_target="tpu_custom_call" | custom-call | flops 12884901888 | bytes 42949672 | tf_op jit(solution)/shard_map/pallas_call | solution.py:19
  544.8 68.2 %shard_map.190 = (bf16[4,768,960]{2,1,0:T(8,128)(2,1)}, f32[4,768,960]{2,1,0:T(8,128)}, f32[4,768,960]{2,1,0:T(8,128)}) custom-call(bf16[4,384,4096]{2,1,0:T(8,128)(2,1)} %shard_map.188.refs_0_, bf16[4,384,4096]{2,1,0:T(8,128)(2,1)} %shard_map.189.refs_1_, bf16[4,960,4096]{2,1,0:T(8,128)(2,1)} %bitcast.81, bf16[4,960,4096]{2,1,0:T(8,128)(2,1)} %bitcast.86), custom_call_target="tpu_custom_call" | custom-call | flops 48318382080 | bytes 161061280 | tf_op jit(solution)/shard_map/pallas_call | solution.py:19
  613.0 20.2 %shard_map.199.refs_1_.refs_3_ = bf16[4,384,4096]{2,1,0:T(8,128)(2,1)} custom-call(bf16[1024,4096]{1,0:T(8,128)(2,1)} %collective-permute-done.16.refs_0_, bf16[1024,4096]{1,0:T(8,128)(2,1)} %collective-permute-done.17.refs_1_, s32[768,2]{1,0:T(8,128)} %get-tuple-element.91.refs_2_, f32[768,2]{1,0:T(8,128)} %get-tuple-element.90.refs_3_), custom_call_target="tpu_custom_call" | custom-call | flops 12884901888 | bytes 42949672 | tf_op jit(solution)/shard_map/pallas_call | solution.py:19
  633.2 40.1 %shard_map.200 = (bf16[4,768,960]{2,1,0:T(8,128)(2,1)}, bf16[4,768,960]{2,1,0:T(8,128)(2,1)}) custom-call(bf16[4,384,4096]{2,1,0:T(8,128)(2,1)} %shard_map.198.refs_0_.refs_2_, bf16[4,384,4096]{2,1,0:T(8,128)(2,1)} %shard_map.199.refs_1_.refs_3_, bf16[4,960,4096]{2,1,0:T(8,128)(2,1)} %refs_2_.5, f32[4,768,960]{2,1,0:T(8,128)} %get-tuple-element.53.refs_3_, ...), custom_call_target="tpu_custom_call" | custom-call | flops 24159191040 | bytes 80530640 | tf_op jit(solution)/shard_map/pallas_call | solution.py:19
  673.2 38.2 %shard_map.201 = (bf16[4,192,4096]{2,1,0:T(8,128)(2,1)}, bf16[4,192,4096]{2,1,0:T(8,128)(2,1)}) custom-call(bf16[4,768,960]{2,1,0:T(8,128)(2,1)} %get-tuple-element.55.refs_0_.refs_1_.refs_5_, bf16[4,768,960]{2,1,0:T(8,128)(2,1)} %get-tuple-element.55.refs_0_.refs_1_.refs_5_, bf16[4,768,960]{2,1,0:T(8,128)(2,1)} %get-tuple-element.56.refs_2_.refs_3_.refs_6_, ...), custom_call_target="tpu_custom_call" | custom-call | flops 24159191040 | bytes 80530640 | tf_op jit(solution)/shard_map/pallas_call | solution.py:19
  713.0 25.2 %shard_map.191 = (bf16[4,192,4096]{2,1,0:T(8,128)(2,1)}, bf16[4,192,4096]{2,1,0:T(8,128)(2,1)}) custom-call(bf16[4,768,960]{2,1,0:T(8,128)(2,1)} %get-tuple-element.42.refs_0_.refs_1_.refs_4_, bf16[4,768,960]{2,1,0:T(8,128)(2,1)} %get-tuple-element.42.refs_0_.refs_1_.refs_4_, bf16[4,960,4096]{2,1,0:T(8,128)(2,1)} %refs_2_.5), custom_call_target="tpu_custom_call" | custom-call | flops 12079595520 | bytes 40265320 | tf_op jit(solution)/shard_map/pallas_call | solution.py:19
  740.2 98.1 %shard_map.210 = (f32[4,960,4096]{2,1,0:T(8,128)}, f32[4,960,4096]{2,1,0:T(8,128)}, f32[4,960,4096]{2,1,0:T(8,128)}) custom-call(bf16[4,384,4096]{2,1,0:T(8,128)(2,1)} %shard_map.188.refs_0_, bf16[4,384,4096]{2,1,0:T(8,128)(2,1)} %shard_map.189.refs_1_, bf16[4,384,4096]{2,1,0:T(8,128)(2,1)} %shard_map.198.refs_0_.refs_2_, ...), custom_call_target="tpu_custom_call" | custom-call | flops 72477573120 | bytes 241591904 | tf_op jit(solution)/shard_map/pallas_call | solution.py:19
  838.4 9.1 collective-permute-done.25.refs_0_
  847.4 272.4 %collective-permute-done.8.refs_0_ = bf16[4,192,4096]{2,1,0:T(8,128)(2,1)} collective-permute-done((bf16[4,192,4096]{2,1,0:T(8,128)(2,1)}, bf16[4,192,4096]{2,1,0:T(8,128)(2,1)}, u32[]{:S(2)}, u32[]{:S(2)}) %collective-permute-start.8) | collective-permute-done | bytes 6291488 | tf_op jit(solution)/shard_map/ppermute | solution.py:345
  1119.8 132.8 %collective-permute-done.9.refs_1_ = bf16[4,192,4096]{2,1,0:T(8,128)(2,1)} collective-permute-done((bf16[4,192,4096]{2,1,0:T(8,128)(2,1)}, bf16[4,192,4096]{2,1,0:T(8,128)(2,1)}, u32[]{:S(2)}, u32[]{:S(2)}) %collective-permute-start.9) | collective-permute-done | bytes 6291488 | tf_op jit(solution)/shard_map/ppermute | solution.py:345
  1252.7 38.5 %shard_map.197 = (bf16[1024,4096]{1,0:T(8,128)(2,1)}, f32[1024,2]{1,0:T(8,128)}) custom-call(bf16[4,192,4096]{2,1,0:T(8,128)(2,1)} %collective-permute-done.8.refs_0_, bf16[4,192,4096]{2,1,0:T(8,128)(2,1)} %collective-permute-done.9.refs_1_, s32[1024,4]{1,0:T(8,128)} %copy.97.refs_2_, f32[1024,2]{1,0:T(8,128)} %copy.98.refs_3_, ...), custom_call_target="tpu_custom_call" | custom-call | flops 25769803776 | bytes 85899344 | tf_op jit(solution)/shard_map/pallas_call | solution.py:19
  1291.2 1.8 multiply_reduce_fusion.1
  1293.1 2.0 add_convert_fusion.refs_7_
  1295.1 41.4 %shard_map.203 = (bf16[1024,4096]{1,0:T(8,128)(2,1)}, f32[1,4096]{1,0:T(1,128)}, f32[1,4096]{1,0:T(1,128)}) custom-call(bf16[4,192,4096]{2,1,0:T(8,128)(2,1)} %collective-permute-done.18.refs_0_, bf16[4,192,4096]{2,1,0:T(8,128)(2,1)} %collective-permute-done.19.refs_1_, s32[1024,4]{1,0:T(8,128)} %copy.97.refs_2_, f32[1024,4096]{1,0:T(8,128)} %shard_map.202.refs_3_, ...), custom_call_target="tpu_custom_call" | custom-call | flops 12884901888 | bytes 42949672 | tf_op jit(solution)/shard_map/pallas_call | solution.py:19
  1338.2 13.4 shard_map.204.refs_0_.refs_1_
  1352.0 4.6 fusion.34
  1356.6 1.7 collective-permute-start.32
  1358.3 1.6 collective-permute-start.28
  1359.9 13.3 shard_map.206.refs_0_.refs_4_
  1375.3 6.1 collective-permute-done.29
  1382.1 13.1 shard_map.205.refs_1_.refs_2_
  1395.3 41.3 %shard_map.208 = (bf16[4,384,960]{2,1,0:T(8,128)(2,1)}, f32[4,384,960]{2,1,0:T(8,128)}, f32[4,384,960]{2,1,0:T(8,128)}) custom-call(bf16[4,192,4096]{2,1,0:T(8,128)(2,1)} %shard_map.204.refs_0_.refs_1_, bf16[4,192,4096]{2,1,0:T(8,128)(2,1)} %shard_map.205.refs_1_.refs_2_, bf16[4,960,4096]{2,1,0:T(8,128)(2,1)} %bitcast.83, bf16[4,960,4096]{2,1,0:T(8,128)(2,1)} %bitcast.88), custom_call_target="tpu_custom_call" | custom-call | flops 24159191040 | bytes 80530640 | tf_op jit(solution)/shard_map/pallas_call | solution.py:19
  1436.5 13.3 shard_map.207.refs_1_.refs_5_
  1449.8 26.8 %shard_map.209 = (bf16[4,384,960]{2,1,0:T(8,128)(2,1)}, bf16[4,384,960]{2,1,0:T(8,128)(2,1)}) custom-call(bf16[4,192,4096]{2,1,0:T(8,128)(2,1)} %shard_map.206.refs_0_.refs_4_, bf16[4,192,4096]{2,1,0:T(8,128)(2,1)} %shard_map.207.refs_1_.refs_5_, bf16[4,960,4096]{2,1,0:T(8,128)(2,1)} %refs_2_.5, f32[4,384,960]{2,1,0:T(8,128)} %get-tuple-element.64.refs_3_, ...), custom_call_target="tpu_custom_call" | custom-call | flops 12079595520 | bytes 40265320 | tf_op jit(solution)/shard_map/pallas_call | solution.py:19
  1476.6 157.9 %shard_map.211 = (f32[4,960,4096]{2,1,0:T(8,128)}, f32[4,960,4096]{2,1,0:T(8,128)}, f32[4,960,4096]{2,1,0:T(8,128)}) custom-call(bf16[4,384,4096]{2,1,0:T(8,128)(2,1)} %shard_map.192.refs_0_, bf16[4,192,4096]{2,1,0:T(8,128)(2,1)} %shard_map.204.refs_0_.refs_1_, ...), custom_call_target="tpu_custom_call", output_to_operand_aliasing={{0}: (12, {}), {1}: (13, {}), {2}: (14, {})} | custom-call | flops 72477573120 | bytes 241591904 | tf_op jit(solution)/shard_map/pallas_call | solution.py:19
  (154 shorter events, 33.7 us)
Async XLA Ops:
  8.8 11.6 copy-start.24
  15.5 30.3 %collective-permute-start.10 = (bf16[1024,4096]{1,0:T(8,128)(2,1)}, bf16[1024,4096]{1,0:T(8,128)(2,1)}, u32[]{:S(2)}, u32[]{:S(2)}) collective-permute-start(bf16[1024,4096]{1,0:T(8,128)(2,1)} %fusion.5.refs_0_), channel_id=1, source_target_pairs={{0,1},{1,0},{2,3},{3,2},{4,5},{5,4},{6,7},{7,6}} | collective-permute-start | bytes 25165832 | tf_op jit(solution)/shard_map/ppermute | solution.py:345
  16.3 51.4 %collective-permute-start.12 = (bf16[1024,4096]{1,0:T(8,128)(2,1)}, bf16[1024,4096]{1,0:T(8,128)(2,1)}, u32[]{:S(2)}, u32[]{:S(2)}) collective-permute-start(bf16[1024,4096]{1,0:T(8,128)(2,1)} %refs_5_.5), channel_id=1, source_target_pairs={{0,1},{1,0},{2,3},{3,2},{4,5},{5,4},{6,7},{7,6}} | collective-permute-start | bytes 25165832 | tf_op jit(solution)/shard_map/ppermute | solution.py:345
  26.2 13.4 copy-start.14
  26.8 12.7 copy-start.16
  35.0 6.4 collective-permute-start.11
  35.5 31.7 %collective-permute-start.3 = (f32[2,3072]{1,0:T(2,128)S(1)}, f32[2,3072]{1,0:T(2,128)S(1)}, u32[]{:S(2)}, u32[]{:S(2)}) collective-permute-start(f32[2,3072]{1,0:T(2,128)S(1)} %pad_maximum_fusion.4), channel_id=1, source_target_pairs={{0,4},{1,5},{2,6},{3,7},{4,0},{5,1},{6,2},{7,3}} | collective-permute-start | bytes 73736 | tf_op jit(solution)/shard_map/ppermute | solution.py:345
  38.0 29.6 %collective-permute-start.2 = (f32[2,3072]{1,0:T(2,128)S(1)}, f32[2,3072]{1,0:T(2,128)S(1)}, u32[]{:S(2)}, u32[]{:S(2)}) collective-permute-start(f32[2,3072]{1,0:T(2,128)S(1)} %pad_maximum_fusion.4), channel_id=1, source_target_pairs={{0,2},{1,3},{2,0},{3,1},{4,6},{5,7},{6,4},{7,5}} | collective-permute-start | bytes 73736 | tf_op jit(solution)/shard_map/ppermute | solution.py:345
  41.4 239.1 %collective-permute-start.1 = (bf16[1024,4096]{1,0:T(8,128)(2,1)}, bf16[1024,4096]{1,0:T(8,128)(2,1)}, u32[]{:S(2)}, u32[]{:S(2)}) collective-permute-start(bf16[1024,4096]{1,0:T(8,128)(2,1)} %fusion.5.refs_0_), channel_id=1, source_target_pairs={{0,4},{1,5},{2,6},{3,7},{4,0},{5,1},{6,2},{7,3}} | collective-permute-start | bytes 25165832 | tf_op jit(solution)/shard_map/ppermute | solution.py:345
  45.8 234.9 %collective-permute-start = (bf16[1024,4096]{1,0:T(8,128)(2,1)}, bf16[1024,4096]{1,0:T(8,128)(2,1)}, u32[]{:S(2)}, u32[]{:S(2)}) collective-permute-start(bf16[1024,4096]{1,0:T(8,128)(2,1)} %fusion.5.refs_0_), channel_id=1, source_target_pairs={{0,2},{1,3},{2,0},{3,1},{4,6},{5,7},{6,4},{7,5}} | collective-permute-start | bytes 25165832 | tf_op jit(solution)/shard_map/ppermute | solution.py:345
  67.2 340.9 %collective-permute-start.14 = (bf16[1024,4096]{1,0:T(8,128)(2,1)}, bf16[1024,4096]{1,0:T(8,128)(2,1)}, u32[]{:S(2)}, u32[]{:S(2)}) collective-permute-start(bf16[1024,4096]{1,0:T(8,128)(2,1)} %refs_5_.5), channel_id=1, source_target_pairs={{0,2},{1,3},{2,0},{3,1},{4,6},{5,7},{6,4},{7,5}} | collective-permute-start | bytes 25165832 | tf_op jit(solution)/shard_map/ppermute | solution.py:345
  67.7 20.2 %collective-permute-start.7 = (f32[2,3072]{1,0:T(2,128)S(1)}, f32[2,3072]{1,0:T(2,128)S(1)}, u32[]{:S(2)}, u32[]{:S(2)}) collective-permute-start(f32[2,3072]{1,0:T(2,128)S(1)} %collective-permute-done.3), channel_id=1, source_target_pairs={{0,1},{1,0},{2,3},{3,2},{4,5},{5,4},{6,7},{7,6}} | collective-permute-start | bytes 73736 | tf_op jit(solution)/shard_map/ppermute | solution.py:345
  67.7 158.1 %collective-permute-start.22 = (f32[2,3072]{1,0:T(2,128)S(1)}, f32[2,3072]{1,0:T(2,128)S(1)}, u32[]{:S(2)}, u32[]{:S(2)}) collective-permute-start(f32[2,3072]{1,0:T(2,128)S(1)} %collective-permute-done.2), channel_id=1, source_target_pairs={{0,4},{1,5},{2,6},{3,7},{4,0},{5,1},{6,2},{7,3}} | collective-permute-start | bytes 73736 | tf_op jit(solution)/shard_map/ppermute | solution.py:345
  87.9 139.6 %collective-permute-start.6 = (f32[2,3072]{1,0:T(2,128)S(1)}, f32[2,3072]{1,0:T(2,128)S(1)}, u32[]{:S(2)}, u32[]{:S(2)}) collective-permute-start(f32[2,3072]{1,0:T(2,128)S(1)} %collective-permute-done.2), channel_id=1, source_target_pairs={{0,1},{1,0},{2,3},{3,2},{4,5},{5,4},{6,7},{7,6}} | collective-permute-start | bytes 73736 | tf_op jit(solution)/shard_map/ppermute | solution.py:345
  225.8 216.8 %collective-permute-start.15 = (bf16[1024,4096]{1,0:T(8,128)(2,1)}, bf16[1024,4096]{1,0:T(8,128)(2,1)}, u32[]{:S(2)}, u32[]{:S(2)}) collective-permute-start(bf16[1024,4096]{1,0:T(8,128)(2,1)} %refs_5_.5), channel_id=1, source_target_pairs={{0,4},{1,5},{2,6},{3,7},{4,0},{5,1},{6,2},{7,3}} | collective-permute-start | bytes 25165832 | tf_op jit(solution)/shard_map/ppermute | solution.py:345
  227.6 52.5 %collective-permute-start.24 = (f32[2,3072]{1,0:T(2,128)S(1)}, f32[2,3072]{1,0:T(2,128)S(1)}, u32[]{:S(2)}, u32[]{:S(2)}) collective-permute-start(f32[2,3072]{1,0:T(2,128)S(1)} %collective-permute-done.22), channel_id=1, source_target_pairs={{0,1},{1,0},{2,3},{3,2},{4,5},{5,4},{6,7},{7,6}} | collective-permute-start | bytes 73736 | tf_op jit(solution)/shard_map/ppermute | solution.py:345
  280.0 183.2 %collective-permute-start.20 = (bf16[4,192,4096]{2,1,0:T(8,128)(2,1)}, bf16[4,192,4096]{2,1,0:T(8,128)(2,1)}, u32[]{:S(2)}, u32[]{:S(2)}) collective-permute-start(bf16[4,192,4096]{2,1,0:T(8,128)(2,1)} %get-tuple-element.60), channel_id=1, source_target_pairs={{0,1},{1,0},{2,3},{3,2},{4,5},{5,4},{6,7},{7,6}} | collective-permute-start | bytes 18874376 | tf_op jit(solution)/shard_map/ppermute | solution.py:345
  280.6 203.9 %collective-permute-start.13 = (bf16[4,192,4096]{2,1,0:T(8,128)(2,1)}, bf16[4,192,4096]{2,1,0:T(8,128)(2,1)}, u32[]{:S(2)}, u32[]{:S(2)}) collective-permute-start(bf16[4,192,4096]{2,1,0:T(8,128)(2,1)} %get-tuple-element.49), channel_id=1, source_target_pairs={{0,1},{1,0},{2,3},{3,2},{4,5},{5,4},{6,7},{7,6}} | collective-permute-start | bytes 18874376 | tf_op jit(solution)/shard_map/ppermute | solution.py:345
  280.6 242.5 %collective-permute-start.5 = (bf16[1024,4096]{1,0:T(8,128)(2,1)}, bf16[1024,4096]{1,0:T(8,128)(2,1)}, u32[]{:S(2)}, u32[]{:S(2)}) collective-permute-start(bf16[1024,4096]{1,0:T(8,128)(2,1)} %collective-permute-done.1.refs_1_), channel_id=1, source_target_pairs={{0,1},{1,0},{2,3},{3,2},{4,5},{5,4},{6,7},{7,6}} | collective-permute-start | bytes 25165832 | tf_op jit(solution)/shard_map/ppermute | solution.py:345
  408.1 116.9 %collective-permute-start.4 = (bf16[1024,4096]{1,0:T(8,128)(2,1)}, bf16[1024,4096]{1,0:T(8,128)(2,1)}, u32[]{:S(2)}, u32[]{:S(2)}) collective-permute-start(bf16[1024,4096]{1,0:T(8,128)(2,1)} %collective-permute-done.refs_0_), channel_id=1, source_target_pairs={{0,1},{1,0},{2,3},{3,2},{4,5},{5,4},{6,7},{7,6}} | collective-permute-start | bytes 25165832 | tf_op jit(solution)/shard_map/ppermute | solution.py:345
  442.6 170.3 %collective-permute-start.16 = (bf16[1024,4096]{1,0:T(8,128)(2,1)}, bf16[1024,4096]{1,0:T(8,128)(2,1)}, u32[]{:S(2)}, u32[]{:S(2)}) collective-permute-start(bf16[1024,4096]{1,0:T(8,128)(2,1)} %collective-permute-done.14.refs_0_), channel_id=1, source_target_pairs={{0,1},{1,0},{2,3},{3,2},{4,5},{5,4},{6,7},{7,6}} | collective-permute-start | bytes 25165832 | tf_op jit(solution)/shard_map/ppermute | solution.py:345
  463.2 149.8 %collective-permute-start.17 = (bf16[1024,4096]{1,0:T(8,128)(2,1)}, bf16[1024,4096]{1,0:T(8,128)(2,1)}, u32[]{:S(2)}, u32[]{:S(2)}) collective-permute-start(bf16[1024,4096]{1,0:T(8,128)(2,1)} %collective-permute-done.15.refs_1_), channel_id=1, source_target_pairs={{0,1},{1,0},{2,3},{3,2},{4,5},{5,4},{6,7},{7,6}} | collective-permute-start | bytes 25165832 | tf_op jit(solution)/shard_map/ppermute | solution.py:345
  484.5 255.0 %collective-permute-start.21 = (bf16[1024,4096]{1,0:T(8,128)(2,1)}, bf16[1024,4096]{1,0:T(8,128)(2,1)}, u32[]{:S(2)}, u32[]{:S(2)}) collective-permute-start(bf16[1024,4096]{1,0:T(8,128)(2,1)} %collective-permute-done.refs_0_), channel_id=1, source_target_pairs={{0,4},{1,5},{2,6},{3,7},{4,0},{5,1},{6,2},{7,3}} | collective-permute-start | bytes 25165832 | tf_op jit(solution)/shard_map/ppermute | solution.py:345
  523.1 324.3 %collective-permute-start.25 = (bf16[1024,4096]{1,0:T(8,128)(2,1)}, bf16[1024,4096]{1,0:T(8,128)(2,1)}, u32[]{:S(2)}, u32[]{:S(2)}) collective-permute-start(bf16[1024,4096]{1,0:T(8,128)(2,1)} %collective-permute-done.14.refs_0_), channel_id=1, source_target_pairs={{0,4},{1,5},{2,6},{3,7},{4,0},{5,1},{6,2},{7,3}} | collective-permute-start | bytes 25165832 | tf_op jit(solution)/shard_map/ppermute | solution.py:345
  711.5 583.6 %collective-permute-start.18 = (bf16[4,192,4096]{2,1,0:T(8,128)(2,1)}, bf16[4,192,4096]{2,1,0:T(8,128)(2,1)}, u32[]{:S(2)}, u32[]{:S(2)}) collective-permute-start(bf16[4,192,4096]{2,1,0:T(8,128)(2,1)} %get-tuple-element.57), channel_id=1, source_target_pairs={{0,2},{1,3},{2,0},{3,1},{4,6},{5,7},{6,4},{7,5}} | collective-permute-start | bytes 18874376 | tf_op jit(solution)/shard_map/ppermute | solution.py:345
  713.0 582.2 %collective-permute-start.19 = (bf16[4,192,4096]{2,1,0:T(8,128)(2,1)}, bf16[4,192,4096]{2,1,0:T(8,128)(2,1)}, u32[]{:S(2)}, u32[]{:S(2)}) collective-permute-start(bf16[4,192,4096]{2,1,0:T(8,128)(2,1)} %get-tuple-element.58), channel_id=1, source_target_pairs={{0,3},{1,2},{2,1},{3,0},{4,7},{5,6},{6,5},{7,4}} | collective-permute-start | bytes 18874376 | tf_op jit(solution)/shard_map/ppermute | solution.py:345
  738.2 381.6 %collective-permute-start.8 = (bf16[4,192,4096]{2,1,0:T(8,128)(2,1)}, bf16[4,192,4096]{2,1,0:T(8,128)(2,1)}, u32[]{:S(2)}, u32[]{:S(2)}) collective-permute-start(bf16[4,192,4096]{2,1,0:T(8,128)(2,1)} %get-tuple-element.43), channel_id=1, source_target_pairs={{0,2},{1,3},{2,0},{3,1},{4,6},{5,7},{6,4},{7,5}} | collective-permute-start | bytes 18874376 | tf_op jit(solution)/shard_map/ppermute | solution.py:345
  739.5 513.1 %collective-permute-start.9 = (bf16[4,192,4096]{2,1,0:T(8,128)(2,1)}, bf16[4,192,4096]{2,1,0:T(8,128)(2,1)}, u32[]{:S(2)}, u32[]{:S(2)}) collective-permute-start(bf16[4,192,4096]{2,1,0:T(8,128)(2,1)} %get-tuple-element.44), channel_id=1, source_target_pairs={{0,3},{1,2},{2,1},{3,0},{4,7},{5,6},{6,5},{7,4}} | collective-permute-start | bytes 18874376 | tf_op jit(solution)/shard_map/ppermute | solution.py:345
  847.4 534.7 %collective-permute-start.23 = (bf16[1024,4096]{1,0:T(8,128)(2,1)}, bf16[1024,4096]{1,0:T(8,128)(2,1)}, u32[]{:S(2)}, u32[]{:S(2)}) collective-permute-start(bf16[1024,4096]{1,0:T(8,128)(2,1)} %collective-permute-done.21.refs_0_), channel_id=1, source_target_pairs={{0,1},{1,0},{2,3},{3,2},{4,5},{5,4},{6,7},{7,6}} | collective-permute-start | bytes 25165832 | tf_op jit(solution)/shard_map/ppermute | solution.py:345
  1119.8 316.7 %collective-permute-start.26 = (bf16[1024,4096]{1,0:T(8,128)(2,1)}, bf16[1024,4096]{1,0:T(8,128)(2,1)}, u32[]{:S(2)}, u32[]{:S(2)}) collective-permute-start(bf16[1024,4096]{1,0:T(8,128)(2,1)} %collective-permute-done.25.refs_0_), channel_id=1, source_target_pairs={{0,1},{1,0},{2,3},{3,2},{4,5},{5,4},{6,7},{7,6}} | collective-permute-start | bytes 25165832 | tf_op jit(solution)/shard_map/ppermute | solution.py:345
  1252.6 38.6 %copy-start.6 = (f32[1024,1]{1,0:T(8,128)S(1)}, f32[1024,1]{1,0:T(8,128)}, u32[]{:S(2)}) copy-start(f32[1024,1]{1,0:T(8,128)} %copy.100) | copy-start | bytes 12292
  1252.6 38.6 %copy-start.7 = (f32[1024,1]{1,0:T(8,128)S(1)}, f32[1024,1]{1,0:T(8,128)}, u32[]{:S(2)}) copy-start(f32[1024,1]{1,0:T(8,128)} %copy.101) | copy-start | bytes 12292
  1252.6 40.4 %copy-start.2 = (f32[1024,16]{1,0:T(8,128)S(1)}, f32[1024,16]{1,0:T(8,128)}, u32[]{:S(2)}) copy-start(f32[1024,16]{1,0:T(8,128)} %copy-done.1) | copy-start | bytes 196612
  1252.6 40.4 %copy-start.3 = (f32[1024,16]{1,0:T(8,128)S(1)}, f32[1024,16]{1,0:T(8,128)}, u32[]{:S(2)}) copy-start(f32[1024,16]{1,0:T(8,128)} %get-tuple-element.87) | copy-start | bytes 196612
  1252.6 40.4 %copy-start.5 = (pred[1024,16]{1,0:T(8,128)(4,1)S(1)}, pred[1024,16]{1,0:T(8,128)(4,1)}, u32[]{:S(2)}) copy-start(pred[1024,16]{1,0:T(8,128)(4,1)} %copy-done.4) | copy-start | bytes 49156
  1252.6 40.4 %copy-start.12 = (s32[1024]{0:T(1024)S(1)}, s32[1024]{0:T(1024)}, u32[]{:S(2)}) copy-start(s32[1024]{0:T(1024)} %param.15) | copy-start | bytes 12292
  1252.7 40.4 %copy-start.15 = (f32[1024]{0:T(1024)S(1)}, f32[1024]{0:T(1024)}, u32[]{:S(2)}) copy-start(f32[1024]{0:T(1024)} %copy-done.14) | copy-start | bytes 12292
  1252.7 40.4 %copy-start.17 = (f32[1024]{0:T(1024)S(1)}, f32[1024]{0:T(1024)}, u32[]{:S(2)}) copy-start(f32[1024]{0:T(1024)} %copy-done.16) | copy-start | bytes 12292
  1252.7 40.4 %copy-start.19 = (s32[1024]{0:T(1024)S(1)}, s32[1024]{0:T(1024)}, u32[]{:S(2)}) copy-start(s32[1024]{0:T(1024)} %param.16) | copy-start | bytes 12292
  1337.3 14.3 copy-start.9
  1337.3 14.3 copy-start.10
  1337.3 14.6 copy-start.8
  1337.3 14.3 collective-permute-start.30
  1351.7 4.9 collective-permute-start.31
  1356.5 1.7 collective-permute-start.27
  1356.6 16.6 %collective-permute-start.32 = (f32[2,4096]{1,0:T(2,128)S(1)}, f32[2,4096]{1,0:T(2,128)S(1)}, u32[]{:S(2)}, u32[]{:S(2)}) collective-permute-start(f32[2,4096]{1,0:T(2,128)S(1)} %fusion.39), channel_id=1, source_target_pairs={{0,2},{1,3},{2,0},{3,1},{4,6},{5,7},{6,4},{7,5}} | collective-permute-start | bytes 98312 | tf_op jit(solution)/shard_map/ppermute | solution.py:345
  1358.3 14.9 collective-permute-start.28
  1373.2 8.2 collective-permute-start.29
  (10 other events, 68.8 us)

commit v2 on v1

v2 whole, which is shorter than its diff:
```python
import jax
import jax.numpy as jnp
from jax import lax
from jax.experimental import pallas as pl
from jax.experimental.pallas import tpu as pltpu
from jax.sharding import PartitionSpec as P

LN_EPS = 1e-5
F32, BF16 = jnp.float32, jnp.bfloat16
VMEM_LIMIT = 60 * 1024 * 1024
ROWS, BOTH_COLS = ((1,), (0,)), ((1,), (1,))


def mm(lhs, rhs, dims=ROWS):
    return lax.dot_general(lhs, rhs, (dims, ((), ())), preferred_element_type=F32)


def call(body, grid, in_specs, out_specs, out_shape, operands, flops, scratch=(), aliases=None):
    return pl.pallas_call(
        body, grid=grid, in_specs=in_specs, out_specs=out_specs, out_shape=out_shape, scratch_shapes=list(scratch),
        input_output_aliases=aliases or {},
        compiler_params=pltpu.CompilerParams(vmem_limit_bytes=VMEM_LIMIT,
                                             dimension_semantics=("arbitrary",) * len(grid)),
        cost_estimate=pl.CostEstimate(flops=flops, transcendentals=0, bytes_accessed=flops // 300))(*operands)


def masked_gate(logits, allowed, choice):
    expert_ids = jnp.arange(logits.shape[-1])
    prob_all = jax.nn.softmax(jnp.where(allowed, logits, -1e30), axis=-1)
    picked = (choice[:, None] == expert_ids[None, :]).astype(F32)
    return jnp.sum(prob_all * picked, axis=-1), prob_all, picked


def gather_rows(tokens, tables, gates, n_exp, cap, into=None, shape=None, row_at=0, col_at=0, after=None):
    n_src, n_part, n_tok = len(tokens), len(tokens[0]), tokens[0][0].shape[0]
    n_col = sum(v.shape[1] for v in tokens[0])
    tile = 512 if n_part > 1 or n_col % 1024 else 1024
    n_slot = n_exp * cap
    extra = [] if gates is None else [gates]
    flat = [v for parts in tokens for v in parts]
    rest = [v for v in (into, after) if v is not None]

    def body(*refs):
        tab_ref, (out_ref, hot_ref) = refs[len(flat)], refs[-2:]

        @pl.when(pl.program_id(0) == 0)
        def _():
            ids = lax.broadcasted_iota(jnp.int32, (n_slot, n_tok), 1)
            for s in range(n_src):
                hot_ref[s] = (ids == tab_ref[:, s:s + 1]).astype(F32).astype(BF16)

        def emit(part):
            for s in range(n_src):
                rows = mm(hot_ref[s], refs[s * n_part + part][...])
                if extra:
                    rows = rows * refs[len(flat) + 1][:, s:s + 1]
                out_ref[:, s * cap:(s + 1) * cap, :] = rows.astype(BF16).reshape(n_exp, cap, tile)

        if n_part == 1:
            emit(0)
        else:
            pl.when(pl.program_id(0) == 0)(lambda: emit(0))
            pl.when(pl.program_id(0) > 0)(lambda: emit(1))

    maps = [lambda j: (0, j)] if n_part == 1 else [lambda j: (0, 0), lambda j: (0, jnp.maximum(j - 1, 0))]
    whole = pl.BlockSpec((n_slot, n_src), lambda j: (0, 0))
    return call(body, (n_col // tile,),
                [pl.BlockSpec((n_tok, tile), m) for _ in tokens for m in maps] + [whole] * (1 + len(extra))
                + [pl.BlockSpec(memory_space=pl.ANY)] * len(rest),
                pl.BlockSpec((n_exp, n_src * cap, tile), lambda j: (0, row_at, j + col_at)),
                jax.ShapeDtypeStruct(shape or (n_exp, n_src * cap, n_col), BF16),
                (*flat, tables, *extra, *rest), 2 * n_src * n_slot * n_tok * n_col,
                [pltpu.VMEM((n_src, n_slot, n_tok), BF16)],
                None if into is None else {len(flat) + 1 + len(extra): 0})


def late_pass(q_rows, w_down, n_first, slopes=None, part=None):
    n_exp, n_row, d_model = q_rows.shape
    d_ff, tile = w_down.shape[1], 512
    n_col = d_model if slopes is None else n_first

    def body(q_ref, w_ref, *refs):
        if slopes is None:
            refs[0][0] = mm(q_ref[0, :, n_first:], w_ref[0, :, n_first:], BOTH_COLS)
        else:
            du = refs[2][0] + mm(q_ref[0], w_ref[0], BOTH_COLS)
            for k in range(2):
                refs[3 + k][0] = (du * refs[k][0]).astype(BF16).T

    act = pl.BlockSpec((1, n_row, tile), lambda e, k: (e, 0, k))
    turn = pl.BlockSpec((1, tile, n_row), lambda e, k: (e, k, 0))
    more = [] if slopes is None else [*slopes, part]
    return call(body, (n_exp, pl.cdiv(d_ff, tile)),
                [pl.BlockSpec((1, n_row, n_col), lambda e, k: (e, 0, 0)), pl.BlockSpec((1, tile, n_col), lambda e, k: (e, k, 0))]
                + [act] * len(more), [turn] * 2 if more else act,
                [jax.ShapeDtypeStruct((n_exp, d_ff, n_row), BF16)] * 2 if more else jax.ShapeDtypeStruct((n_exp, n_row, d_ff), F32),
                (q_rows, w_down, *more), 2 * n_exp * n_row * n_col * d_ff)


def stack_rows(refs):
    return refs[0][0] if len(refs) == 1 else jnp.concatenate([r[0] for r in refs], axis=0)


def up_pass(h_sets, q_sets, weights, saved=None, plain=True):
    h_sets, q_sets, saved = list(h_sets or []), list(q_sets or []), list(saved or [])
    sets = h_sets or q_sets
    groups = [[i] for i in range(len(sets))] if sets[0].shape[1] >= 256 else [list(range(len(sets)))]
    n_exp, _, d_model = sets[0].shape
    n_row = sum(v.shape[1] for v in sets)
    d_ff, tile = weights[2].shape[1], 512
    n_h, n_q = len(h_sets), len(q_sets)
    w_in = ([weights[0], weights[1]] if n_h else []) + ([weights[2]] if n_q else [])
    n_half = (1 if n_h else 0) + (2 if n_q else 0)
    n_slope = 0 if n_q else 2

    def body(*refs):
        refs = list(refs)
        take = lambda n: [refs.pop(0) for _ in range(n)]
        h_refs, q_refs, w_refs, saved_refs = take(n_h), take(n_q), take(len(w_in)), take(len(saved))
        flat, turned, slopes = take(n_half if plain else 0), take(n_half), take(n_slope)
        at = 0
        for group in groups:
            size = sum(sets[i].shape[1] for i in group)
            rows = pl.ds(at, size)
            at += size
            halves = []
            if n_h:
                h = stack_rows([h_refs[i] for i in group])
                a = mm(h, w_refs[0][0], BOTH_COLS)
                b = mm(h, w_refs[1][0], BOTH_COLS)
                sig = jax.nn.sigmoid(a)
                silu = a * sig
                halves.append(silu * b)
                slope = b * sig * (1.0 + a * (1.0 - sig))
            else:
                slope, silu = saved_refs[0][0, rows], saved_refs[1][0, rows]
            if n_q:
                du = mm(stack_rows([q_refs[i] for i in group]), w_refs[-1][0], BOTH_COLS)
                halves += [du * slope, du * silu]
            else:
                slopes[0][0, rows] = slope
                slopes[1][0, rows] = silu
            for n, value in enumerate(halves):
                value = value.astype(BF16)
                if plain:
                    flat[n][0, rows] = value
                turned[n][0, :, rows] = value.T

    row = lambda v: pl.BlockSpec((1, v.shape[1], d_model), lambda e, k: (e, 0, 0))
    wide = pl.BlockSpec((1, tile, d_model), lambda e, k: (e, k, 0))
    act = pl.BlockSpec((1, n_row, tile), lambda e, k: (e, 0, k))
    turn = pl.BlockSpec((1, tile, n_row), lambda e, k: (e, k, 0))
    n_flat = n_half if plain else 0
    out = call(body, (n_exp, pl.cdiv(d_ff, tile)),
               [row(v) for v in h_sets + q_sets] + [wide] * len(w_in) + [act] * len(saved),
               [act] * n_flat + [turn] * n_half + [act] * n_slope,
               [jax.ShapeDtypeStruct((n_exp, n_row, d_ff), BF16)] * n_flat + [jax.ShapeDtypeStruct((n_exp, d_ff, n_row), BF16)] * n_half
               + [jax.ShapeDtypeStruct((n_exp, n_row, d_ff), F32)] * n_slope, (*h_sets, *q_sets, *w_in, *saved),
               2 * n_exp * n_row * d_model * d_ff * len(w_in))
    return out[:n_flat], out[n_flat:n_flat + n_half], out[n_flat + n_half:]


def down_pass(inner, d_gate, d_up, weights, cap, picks):
    has_o, has_d = inner is not None, d_gate is not None
    acts = ([inner] if has_o else []) + ([d_gate, d_up] if has_d else [])
    w_in = ([weights[2]] if has_o else []) + ([weights[0], weights[1]] if has_d else [])
    n_exp, _, d_ff = acts[0].shape
    d_model, tile, n_src = weights[2].shape[2], 2048, len(picks)

    def body(*refs):
        refs = list(refs)
        take = lambda n: [refs.pop(0) for _ in range(n)]
        rows = [take(n_src) for _ in acts]
        w_refs = take(len(acts))
        if has_o:
            out = mm(stack_rows(rows[0]), w_refs[0][0]).astype(BF16)
            for s in range(n_src):
                refs.pop(0)[0] = out[s * cap:(s + 1) * cap]
        if has_d:
            back = (mm(stack_rows(rows[-2]), w_refs[-2][0]) + mm(stack_rows(rows[-1]), w_refs[-1][0])).astype(BF16)
            for s in range(n_src):
                refs.pop(0)[0] = back[s * cap:(s + 1) * cap]

    wide = pl.BlockSpec((1, d_ff, tile), lambda e, j: (e, 0, j))
    act = [pl.BlockSpec((1, cap, d_ff), lambda e, j, p=p: (e, p, 0)) for p in picks]
    n_out = n_src * (has_o + has_d)
    return call(body, (n_exp, d_model // tile),
                act * len(acts) + [wide] * len(w_in),
                [pl.BlockSpec((1, cap, tile), lambda e, j: (e, 0, j))] * n_out,
                [jax.ShapeDtypeStruct((n_exp, cap, d_model), BF16)] * n_out,
                (*[a for a in acts for _ in picks], *w_in),
                2 * n_exp * n_src * cap * d_model * d_ff * len(acts))


def weight_grads(jobs, tile):
    n_exp, _, d_model = jobs[0][1][0].shape
    d_ff = jobs[0][0][0].shape[1]
    operands, specs, where, shared = [], [], [], {}

    def put(value, spec):
        if id(value) not in shared:
            shared[id(value)] = len(operands)
            operands.append(value)
            specs.append(spec)
        return shared[id(value)]

    row = lambda v: pl.BlockSpec((1, v.shape[1], tile), lambda e, i: (e, 0, i))
    act = lambda v: pl.BlockSpec((1, d_ff, v.shape[2]), lambda e, i: (e, 0, 0))
    wide = pl.BlockSpec((1, d_ff, tile), lambda e, i: (e, 0, i))
    aliases = {}
    for n, (acts, rows, before) in enumerate(jobs):
        at = [put(v, act(v)) for v in acts], [put(v, row(v)) for v in rows], None if before is None else put(before, wide)
        where.append(at)
        if before is not None:
            aliases[at[2]] = n
    n_rows = [sum(v.shape[1] for v in rows) for _, rows, _ in jobs]

    def body(*refs):
        ins, outs = refs[:len(operands)], refs[len(operands):]
        for (acts, rows, before), out in zip(where, outs):
            total = mm(jnp.concatenate([ins[r][0] for r in acts], axis=1), stack_rows([ins[r] for r in rows]))
            out[0] = total if before is None else ins[before][0] + total

    return call(body, (n_exp, d_model // tile), specs, [wide] * len(jobs),
                [jax.ShapeDtypeStruct((n_exp, d_ff, d_model), F32)] * len(jobs), operands,
                2 * n_exp * sum(n_rows) * d_model * d_ff, (), aliases)


def lane_sums(value):
    return sum(value[:, i:i + 128] for i in range(0, value.shape[1], 128))


def one_hot(pos, n_slot):
    return (lax.broadcasted_iota(jnp.int32, (pos.shape[0], n_slot), 1) == pos).astype(F32).astype(BF16)


def combine_out(blocks, pos, gates, base, tok_dy, dg_base=None):
    n_blk = len(blocks)
    n_exp, cap, d_model = blocks[0].shape
    n_tok, tile, step = tok_dy.shape[0], 512, 256
    n_slot = n_exp * cap
    extra = [] if dg_base is None else [dg_base]

    def body(*refs):
        blk = refs[:n_blk]
        pos_ref, gate_ref, base_ref, dy_ref = refs[n_blk:n_blk + 4]
        out_ref, dg_ref, hot_one, hot_two, sum_one, sum_two = refs[-6:]

        @pl.when(pl.program_id(0) == 0)
        def _():
            sum_one[...] = jnp.zeros_like(sum_one)
            sum_two[...] = jnp.zeros_like(sum_two)
            for f in range(n_blk):
                hot_one[f] = one_hot(pos_ref[:, f:f + 1], n_slot)
                hot_two[f] = one_hot(pos_ref[:, n_blk + f:n_blk + f + 1], n_slot)

        def col(j):
            at = pl.ds(j * step, step)
            o_one = sum(mm(hot_one[f], blk[f][:, :, at].reshape(n_slot, step)) for f in range(n_blk))
            o_two = sum(mm(hot_two[f], blk[f][:, :, at].reshape(n_slot, step)) for f in range(n_blk))
            dy = dy_ref[:, at].astype(F32)
            mix = gate_ref[:, 0:1] * o_one + gate_ref[:, 1:2] * o_two
            out_ref[:, at] = (base_ref[:, at].astype(F32) + mix).astype(out_ref.dtype)
            sum_one[...] += lane_sums(dy * o_one)
            sum_two[...] += lane_sums(dy * o_two)

        [col(j) for j in range(tile // step)]

        @pl.when(pl.program_id(0) == pl.num_programs(0) - 1)
        def _():
            for k, total in enumerate((sum_one, sum_two)):
                dg = jnp.sum(total[...], axis=1, keepdims=True)
                dg_ref[:, k:k + 1] = refs[n_blk + 4][:, k:k + 1] + dg if extra else dg

    tok = pl.BlockSpec((n_tok, tile), lambda j: (0, j))
    small = lambda n: pl.BlockSpec((n_tok, n), lambda j: (0, 0))
    return call(body, (d_model // tile,),
                [pl.BlockSpec((n_exp, cap, tile), lambda j: (0, 0, j))] * n_blk + [small(2 * n_blk), small(2), tok, tok]
                + [small(2)] * len(extra), [tok, small(2)],
                [jax.ShapeDtypeStruct((n_tok, d_model), BF16 if extra else F32), jax.ShapeDtypeStruct((n_tok, 2), F32)],
                (*blocks, pos, gates, base, tok_dy, *extra), 4 * n_tok * n_blk * n_slot * d_model,
                [pltpu.VMEM((n_blk, n_tok, n_slot), BF16)] * 2 + [pltpu.VMEM((n_tok, 128), F32)] * 2)


def pair_hot(hot_ref, pos_ref, n_blk, n_slot):
    ids = lax.broadcasted_iota(jnp.int32, (pos_ref.shape[0], n_slot), 1)
    for f in range(n_blk):
        hit = (ids == pos_ref[:, f:f + 1]) | (ids == pos_ref[:, n_blk + f:n_blk + f + 1])
        hot_ref[f] = hit.astype(F32).astype(BF16)


def combine_part(blocks, pos):
    n_blk = len(blocks)
    n_exp, cap, d_model = blocks[0].shape
    n_tok, tile, step = pos.shape[0], 512, 256
    n_slot = n_exp * cap

    def body(*refs):
        blk, (pos_ref, out_ref, hot_ref) = refs[:n_blk], refs[n_blk:]

        @pl.when(pl.program_id(0) == 0)
        def _():
            pair_hot(hot_ref, pos_ref, n_blk, n_slot)

        def col(j):
            at = pl.ds(j * step, step)
            out_ref[:, at] = sum(mm(hot_ref[f], blk[f][:, :, at].reshape(n_slot, step)) for f in range(n_blk))

        [col(j) for j in range(tile // step)]

    return call(body, (d_model // tile,),
                [pl.BlockSpec((n_exp, cap, tile), lambda j: (0, 0, j))] * n_blk + [pl.BlockSpec((n_tok, 2 * n_blk), lambda j: (0, 0))],
                pl.BlockSpec((n_tok, tile), lambda j: (0, j)), jax.ShapeDtypeStruct((n_tok, d_model), F32),
                (*blocks, pos), 2 * n_tok * n_blk * n_slot * d_model, [pltpu.VMEM((n_blk, n_tok, n_slot), BF16)])


def combine_back(blocks, pos, part, tok_x, tok_dy, stats, d_logits, router, ln_weight):
    n_blk = len(blocks)
    n_exp, cap, d_model = blocks[0].shape
    n_tok, tile, step = tok_x.shape[0], 512, 256
    n_slot, n_tile = n_exp * cap, d_model // 512

    def body(*refs):
        blk = refs[:n_blk]
        (pos_ref, part_ref, x_ref, dy_ref, stat_ref, dl_ref, rt_ref, lnw_ref,
         dx_ref, dw_ref, db_ref, hot_ref, gh_ref, s1_ref, s2_ref, m1_ref, m2_ref) = refs[n_blk:]
        phase, j = pl.program_id(0), pl.program_id(1)

        @pl.when((phase == 0) & (j == 0))
        def _():
            s1_ref[...] = jnp.zeros_like(s1_ref)
            s2_ref[...] = jnp.zeros_like(s2_ref)
            pair_hot(hot_ref, pos_ref, n_blk, n_slot)

        @pl.when(phase == 0)
        def _():
            def col(i):
                at = pl.ds(i * step, step)
                grad = sum(mm(hot_ref[f], blk[f][:, :, at].reshape(n_slot, step)) for f in range(n_blk))
                grad = mm(dl_ref[...], rt_ref[:, at]) + (part_ref[:, at] + grad)
                gh_ref[j, :, at] = grad
                x_hat = (x_ref[:, at].astype(F32) - stat_ref[:, 0:1]) * stat_ref[:, 1:2]
                scaled = grad * lnw_ref[:, at].astype(F32)
                s1_ref[...] += lane_sums(scaled)
                s2_ref[...] += lane_sums(scaled * x_hat)
                dw_ref[:, at] = jnp.sum(grad * x_hat, axis=0, keepdims=True)
                db_ref[:, at] = jnp.sum(grad, axis=0, keepdims=True)

            [col(i) for i in range(tile // step)]

        @pl.when((phase == 1) & (j == 0))
        def _():
            m1_ref[...] = jnp.sum(s1_ref[...], axis=1, keepdims=True) / d_model
            m2_ref[...] = jnp.sum(s2_ref[...], axis=1, keepdims=True) / d_model

        @pl.when(phase == 1)
        def _():
            x_hat = (x_ref[...].astype(F32) - stat_ref[:, 0:1]) * stat_ref[:, 1:2]
            scaled = gh_ref[j] * lnw_ref[...].astype(F32)
            d_ln = stat_ref[:, 1:2] * (scaled - m1_ref[...] - x_hat * m2_ref[...])
            dx_ref[...] = (dy_ref[...].astype(F32) + d_ln).astype(BF16)

    last = n_tile - 1
    early = lambda p, j: j * (1 - p) + last * p
    tok = pl.BlockSpec((n_tok, tile), lambda p, j: (0, j))
    tok_early = pl.BlockSpec((n_tok, tile), lambda p, j: (0, early(p, j)))
    tok_late = pl.BlockSpec((n_tok, tile), lambda p, j: (0, j * p))
    wide = lambda n: pl.BlockSpec((n, tile), lambda p, j: (0, j))
    wide_early = lambda n: pl.BlockSpec((n, tile), lambda p, j: (0, early(p, j)))
    small = lambda n: pl.BlockSpec((n_tok, n), lambda p, j: (0, 0))
    return call(body, (2, n_tile),
                [pl.BlockSpec((n_exp, cap, tile), lambda p, j: (0, 0, early(p, j)))] * n_blk
                + [small(2 * n_blk), tok_early, tok, tok_late, small(2), small(router.shape[0]), wide(router.shape[0]), wide(1)],
                [tok_late, wide_early(1), wide_early(1)],
                [jax.ShapeDtypeStruct((n_tok, d_model), BF16)] + [jax.ShapeDtypeStruct((1, d_model), F32)] * 2,
                (*blocks, pos, part, tok_x, tok_dy, stats, d_logits, router, ln_weight), 2 * n_tok * n_blk * n_slot * d_model,
                [pltpu.VMEM((n_blk, n_tok, n_slot), BF16), pltpu.VMEM((n_tile, n_tok, tile), F32)]
                + [pltpu.VMEM((n_tok, 128), F32)] * 2 + [pltpu.VMEM((n_tok, 1), F32)] * 2)


FLIPS = {'x': (0, 2), 'y': (1, 0), 'c': (0, 1), 'd': (0, 3)}


def solution(mesh):
    n_dp, n_ep = mesh.shape['dp'], mesh.shape['ep']
    tok_spec = P(('dp', 'ep'), None)
    row_spec = P(('dp', 'ep'))
    exp_spec = P('ep', None, None)

    def swap(name, value, flips=None):
        flip_dp, flip_ep = flips or FLIPS[name[-1]]
        pairs = [(d * n_ep + e, (d ^ flip_dp) * n_ep + (e ^ flip_ep)) for d in range(n_dp) for e in range(n_ep)]
        return lax.ppermute(value, ('dp', 'ep'), pairs)

    def local_step(tok_x, tok_dy, exp_first, exp_second, eligible, slot_first, slot_second,
                   ln_weight, ln_bias, router, w_gate, w_up, w_down):
        n_local, d_model = tok_x.shape
        n_exp = eligible.shape[1]
        local_exp = w_gate.shape[0]
        cap = 3 * n_local // n_exp
        n_slot = local_exp * cap
        me = lax.axis_index('ep')
        weights = (jnp.swapaxes(w_gate, 1, 2), jnp.swapaxes(w_up, 1, 2), w_down)

        x_float = tok_x.astype(F32)
        mean = jnp.mean(x_float, axis=-1, keepdims=True)
        centered = x_float - mean
        inv_std = lax.rsqrt(jnp.mean(centered * centered, axis=-1, keepdims=True) + LN_EPS)
        hidden = (centered * inv_std * ln_weight.astype(F32) + ln_bias.astype(F32)).astype(BF16)
        logits = jnp.dot(hidden, router, preferred_element_type=F32)
        expert_ids = jnp.arange(n_exp)
        allowed = eligible > 0
        gate_one, prob_one, pick_one = masked_gate(logits, allowed, exp_first)
        gate_two, prob_two, pick_two = masked_gate(logits, allowed & (expert_ids[None, :] != exp_first[:, None]), exp_second)
        pos_one = jnp.where(slot_first >= 0, exp_first * cap + slot_first, -1)
        pos_two = jnp.where(slot_second >= 0, exp_second * cap + slot_second, -1)
        row_ids = jnp.arange(n_exp * cap)
        hit_one = pos_one[:, None] == row_ids[None, :]
        hit_two = pos_two[:, None] == row_ids[None, :]
        slot_tok = jnp.max(jnp.where(hit_one | hit_two, jnp.arange(n_local)[:, None], -1), axis=0).astype(F32)
        slot_gate = jnp.sum(jnp.where(hit_one, gate_one[:, None], 0.0) + jnp.where(hit_two, gate_two[:, None], 0.0), axis=0)
        meta = jnp.stack([slot_tok, slot_gate])

        def columns(*tables):
            mine = [lax.dynamic_slice(t, (0, me * n_slot), (2, n_slot)) for t in tables]
            both = jnp.stack(mine, axis=-1)
            return both[0].astype(jnp.int32), both[1]

        def spread(name, value):
            from_x = swap(name + '_x', value)
            from_y = swap(name + '_y', value)
            from_d = swap(name + '_xy', from_x)
            return [(v, swap(name + end, v)) for v, end in
                    ((value, '_c'), (from_x, '_xc'), (from_y, '_yc'), (from_d, '_dc'))]

        (m_a, m_x, m_y, m_d) = spread('m', meta)
        (h_a, h_x, h_y, h_d) = spread('h', hidden)
        first = spread('f', tok_dy[:, :512])
        rest = spread('g', tok_dy[:, 512:])
        g_a, g_x, g_y, g_d = ([(f, g) for f, g in zip(*both)] for both in zip(first, rest))
        h_a, h_x, h_y, h_d = ([(v,) for v in both] for both in (h_a, h_x, h_y, h_d))

        def gath(name, toks, tables):
            tab, gts = columns(*tables)
            return gather_rows(toks, tab, gts if name[-1] == 'q' else None, local_exp, cap)

        ha, qa = [gath('a_gath', h_a, m_a)], [gath('a_gq', g_a, m_a)]
        act_a, (ut_a, gt_a, vt_a), _ = up_pass(ha, qa, weights)
        o_a0, o_a1, b_a0, b_a1 = down_pass(*act_a, weights, cap, (0, 1))
        m_p, m_r = (m_x[0], m_y[0]), (m_x[1], m_y[1])
        hxy = [gath('p_gh', (h_x[0], h_y[0]), m_p), gath('r_gh', (h_x[1], h_y[1]), m_r)]
        (u_xy,), (ut_xy,), slopes = up_pass(hxy, None, weights)
        o_x0, o_x1 = down_pass(u_xy, None, None, weights, cap, (0, 2))
        qxy = [gath('p_gq', (g_x[0], g_y[0]), m_p), gath('r_gq', (g_x[1], g_y[1]), m_r)]
        d_xy, (gt_xy, vt_xy), _ = up_pass(None, qxy, weights, slopes)
        b_x0, b_x1 = down_pass(None, *d_xy, weights, cap, (0, 2))
        part, = weight_grads([((vt_xy, vt_a), hxy + ha, None)], 1024)
        hd = [gath('d%d_gh' % i, h_d[i:i + 1], m_d[i:i + 1]) for i in range(2)]
        _, (ut_d,), slopes = up_pass(hd, None, weights, plain=False)
        whole, qd = (local_exp, 2 * cap, d_model), None
        cols_d = [columns(m_d[0]), columns(m_d[1]), columns(*m_d)]
        stats = jnp.concatenate([mean, inv_std], axis=1)
        for i in range(2):
            qd = gather_rows([g_d[i][1:]], *cols_d[i], local_exp, cap, qd, whole, i, 1)
        du = late_pass(qd, w_down, 512)
        qd = gather_rows([g[:1] for g in g_d], *cols_d[2], local_exp, cap, qd, whole, after=du)
        gt_d, vt_d = late_pass(qd, w_down, 512, slopes, du)
        qd = [qd]
        dw_down, dw_gate, dw_up = weight_grads([
            ((ut_xy, ut_a, ut_d), qxy + qa + qd, None),
            ((gt_xy, gt_a, gt_d), hxy + ha + hd, None),
            ((vt_d,), hd, part)], 512)

        outs = [o_a0, swap('o_c', o_a1), swap('o_x', o_x0), swap('o_d', o_x1)]
        backs = [b_a0, swap('b_c', b_a1), swap('b_x', b_x0), swap('b_d', b_x1)]

        def slots(flips):
            cols = [(p, p - (me ^ f) * n_slot) for p in (pos_one, pos_two) for f in flips]
            return jnp.stack([jnp.where(p < 0, -1, at) for p, at in cols], axis=-1)

        near, far = slots((0, 1)), slots((2, 3))
        gates = jnp.stack([gate_one, gate_two], axis=-1)
        mix, dgate = combine_out(outs[:2], near, gates, tok_x, tok_dy)
        out_tok, dgate = combine_out(outs[2:], far, gates, mix, tok_dy, dgate)
        d_logits = ((dgate[:, 0] * gate_one)[:, None] * (pick_one - prob_one)
                    + (dgate[:, 1] * gate_two)[:, None] * (pick_two - prob_two)).astype(BF16)
        d_router = jnp.einsum('te,td->ed', d_logits, hidden, preferred_element_type=F32)

        def sum_all(name, value):
            for end in ('_c', '_y', '_x'):
                value = value + swap(name + end, value)
            return value

        d_router = sum_all('r', d_router)
        part_back = combine_part(backs[:2], near)
        dx_tok, d_lnw, d_lnb = combine_back(backs[2:], far, part_back, tok_x, tok_dy,
                                            stats, d_logits, router.T, ln_weight[None, :])
        d_ln = jnp.concatenate([d_lnw, d_lnb], axis=0)
        terms = [d_ln] + [swap('l%d' % f, d_ln, divmod(f, n_ep)) for f in range(1, n_dp * n_ep)]
        while len(terms) > 1:
            terms = [a + b for a, b in zip(terms[::2], terms[1::2])]
        d_ln = terms[0]
        return (out_tok, dx_tok, jnp.swapaxes(dw_gate, 1, 2), jnp.swapaxes(dw_up, 1, 2), dw_down, d_router.T, d_ln[0], d_ln[1])

    return jax.shard_map(
        local_step, mesh=mesh,
        in_specs=(tok_spec, tok_spec, row_spec, row_spec, tok_spec, row_spec, row_spec,
                  P(), P(), P(), exp_spec, exp_spec, exp_spec),
        out_specs=(tok_spec, tok_spec, exp_spec, exp_spec, exp_spec, P(), P(), P()),
        check_vma=False)
```

time: 1640 us -> 1820 us (1.11)
  waiting for transfers between devices: 631 us -> 870 us
  Pallas kernels: 916 us -> 843 us
    ppermute x33 -> x44, waiting for transfers between devices: 631 us -> 870 us  [swap(): return lax.ppermute(value, ('dp', 'ep'), pairs)]
    pallas_call x24 -> x26, Pallas kernels: 916 us -> 843 us  [call(): pl.pallas_call(body, grid=grid, in_specs=in_specs, out_specs=out_specs, o...]
  transfers between devices with their start and end apart: 33 -> 44, of which waited for: 7 -> 12; matrix products, arithmetic and copies ran while one was open for 3% -> 3% of each run, Pallas kernels for 44% -> 35%
where the time goes in v2:
time: 1820 us; the launch traced here: 1810 us
  waiting for transfers between devices  870 us (48%)
  Pallas kernels  843 us (46%)
  other arithmetic  32.7 us (2%)
  starting transfers between devices  30.5 us (2%)
  local copies, waits for them, and re-layouts  22.3 us (1%)
    ppermute x44, waiting for transfers between devices, swap(): return lax.ppermute(value, ('dp', 'ep'), pairs)  870 us
    pallas_call x26, Pallas kernels, call(): pl.pallas_call(body, grid=grid, in_specs=in_specs, out_specs=out_specs, o...  843 us
  transfers between devices with their start and end apart: 44, of which 12 were waited for; matrix products, arithmetic and copies ran while one was open for 3% of the time, Pallas kernels for 35%

profile of v2, /device:TPU:0, one launch (start us, length us, event | category | flops | bytes accessed | tf_op | source)
XLA Modules:
  0.0 1810.1 jit_solution(16085284726303801238)
XLA Ops:
  0.6 7.0 slice.67.refs_1_
  9.7 2.3 fusion.2
  12.1 6.2 fusion.5.refs_0_
  18.6 2.7 collective-permute-start.16
  22.9 5.9 fusion.29
  32.3 5.3 add_reduce_fusion
  37.6 3.8 select_reduce_fusion
  44.2 136.2 %collective-permute-done.2 = f32[2,3072]{1,0:T(2,128)S(1)} collective-permute-done((f32[2,3072]{1,0:T(2,128)S(1)}, f32[2,3072]{1,0:T(2,128)S(1)}, u32[]{:S(2)}, u32[]{:S(2)}) %collective-permute-start.2) | collective-permute-done | bytes 24608 | tf_op jit(solution)/shard_map/ppermute | solution.py:393
  180.5 1.8 collective-permute-start.17
  182.5 1.8 collective-permute-start.27
  184.3 19.8 %shard_map.193.refs_1_.refs_5_ = bf16[4,384,4096]{2,1,0:T(8,128)(2,1)} custom-call(bf16[1024,512]{1,0:T(8,128)(2,1)} %copy-done.10, bf16[1024,3584]{1,0:T(8,128)(2,1)} %slice.67.refs_1_, bf16[1024,512]{1,0:T(8,128)(2,1)} %collective-permute-done.12.refs_2_, bf16[1024,3584]{1,0:T(8,128)(2,1)} %collective-permute-done.13.refs_3_, ...), custom_call_target="tpu_custom_call" | custom-call | flops 12884901888 | bytes 42949672 | tf_op jit(solution)/shard_map/pallas_call | solution.py:19
  204.1 2.0 collective-permute-done.3
  206.9 18.3 %shard_map.192.refs_0_.refs_4_.refs_12_ = bf16[4,384,4096]{2,1,0:T(8,128)(2,1)} custom-call(bf16[1024,4096]{1,0:T(8,128)(2,1)} %fusion.5.refs_0_, bf16[1024,4096]{1,0:T(8,128)(2,1)} %collective-permute-done.10.refs_1_, s32[768,2]{1,0:T(8,128)} %get-tuple-element.103.refs_2_.refs_4_), custom_call_target="tpu_custom_call" | custom-call | flops 12884901888 | bytes 42949672 | tf_op jit(solution)/shard_map/pallas_call | solution.py:19
  228.7 58.9 %shard_map.194 = (bf16[4,384,960]{2,1,0:T(8,128)(2,1)}, bf16[4,384,960]{2,1,0:T(8,128)(2,1)}, bf16[4,384,960]{2,1,0:T(8,128)(2,1)}, bf16[4,960,384]{2,1,0:T(8,12...) custom-call(bf16[4,384,4096]{2,1,0:T(8,128)(2,1)} %shard_map.192.refs_0_.refs_4_.refs_12_, ...), custom_call_target="tpu_custom_call" | custom-call | flops 36238786560 | bytes 120795952 | tf_op jit(solution)/shard_map/pallas_call | solution.py:19
  289.8 51.5 %shard_map.195 = (bf16[4,192,4096]{2,1,0:T(8,128)(2,1)}, bf16[4,192,4096]{2,1,0:T(8,128)(2,1)}, bf16[4,192,4096]{2,1,0:T(8,128)(2,1)}, bf16[4,192,4096]{2,1,0:T(8,128)(2,1)}) custom-call(bf16[4,384,960]{2,1,0:T(8,128)(2,1)} %get-tuple-element.48.refs_0_.refs_1_, bf16[4,384,960]{2,1,0:T(8,128)(2,1)} %get-tuple-element.48.refs_0_.refs_1_, ...), custom_call_target="tpu_custom_call" | custom-call | flops 36238786560 | bytes 120795952 | tf_op jit(solution)/shard_map/pallas_call | solution.py:19
  341.5 46.3 %collective-permute-done.18.refs_3_ = bf16[1024,3584]{1,0:T(8,128)(2,1)} collective-permute-done((bf16[1024,3584]{1,0:T(8,128)(2,1)}, bf16[1024,3584]{1,0:T(8,128)(2,1)}, u32[]{:S(2)}, u32[]{:S(2)}) %collective-permute-start.18) | collective-permute-done | bytes 7340064 | tf_op jit(solution)/shard_map/ppermute | solution.py:393
  387.9 179.8 %collective-permute-done.1.refs_1_ = bf16[1024,4096]{1,0:T(8,128)(2,1)} collective-permute-done((bf16[1024,4096]{1,0:T(8,128)(2,1)}, bf16[1024,4096]{1,0:T(8,128)(2,1)}, u32[]{:S(2)}, u32[]{:S(2)}) %collective-permute-start.1) | collective-permute-done | bytes 8388640 | tf_op jit(solution)/shard_map/ppermute | solution.py:393
  576.9 147.0 %collective-permute-done.32.refs_0_ = bf16[1024,3584]{1,0:T(8,128)(2,1)} collective-permute-done((bf16[1024,3584]{1,0:T(8,128)(2,1)}, bf16[1024,3584]{1,0:T(8,128)(2,1)}, u32[]{:S(2)}, u32[]{:S(2)}) %collective-permute-start.32) | collective-permute-done | bytes 7340064 | tf_op jit(solution)/shard_map/ppermute | solution.py:393
  731.9 19.7 %shard_map.198.refs_0_.refs_3_ = bf16[4,384,4096]{2,1,0:T(8,128)(2,1)} custom-call(bf16[1024,512]{1,0:T(8,128)(2,1)} %collective-permute-done.15.refs_0_, bf16[1024,3584]{1,0:T(8,128)(2,1)} %collective-permute-done.16.refs_1_, bf16[1024,512]{1,0:T(8,128)(2,1)} %copy-done.27, bf16[1024,3584]{1,0:T(8,128)(2,1)} %collective-permute-done.18.refs_3_, ...), custom_call_target="tpu_custom_call" | custom-call | flops 12884901888 | bytes 42949672 | tf_op jit(solution)/shard_map/pallas_call | solution.py:19
  751.6 18.3 %shard_map.188.refs_0_.refs_2_.refs_10_ = bf16[4,384,4096]{2,1,0:T(8,128)(2,1)} custom-call(bf16[1024,4096]{1,0:T(8,128)(2,1)} %collective-permute-done.refs_0_, bf16[1024,4096]{1,0:T(8,128)(2,1)} %collective-permute-done.1.refs_1_, s32[768,2]{1,0:T(8,128)} %get-tuple-element.101.refs_2_.refs_4_), custom_call_target="tpu_custom_call" | custom-call | flops 12884901888 | bytes 42949672 | tf_op jit(solution)/shard_map/pallas_call | solution.py:19
  769.9 11.2 shard_map.207.refs_3_
  781.1 19.7 %shard_map.202.refs_3_ = f32[1024,4096]{1,0:T(8,128)} custom-call(bf16[4,192,4096]{2,1,0:T(8,128)(2,1)} %get-tuple-element.62.refs_0_, bf16[4,192,4096]{2,1,0:T(8,128)(2,1)} %collective-permute-done.25.refs_1_, s32[1024,4]{1,0:T(8,128)} %copy.101.refs_2_), custom_call_target="tpu_custom_call" | custom-call | flops 12884901888 | bytes 42949672 | tf_op jit(solution)/shard_map/pallas_call | solution.py:19
  802.8 19.8 %shard_map.199.refs_1_.refs_4_ = bf16[4,384,4096]{2,1,0:T(8,128)(2,1)} custom-call(bf16[1024,512]{1,0:T(8,128)(2,1)} %copy-done.29, bf16[1024,3584]{1,0:T(8,128)(2,1)} %collective-permute-done.20.refs_1_, bf16[1024,512]{1,0:T(8,128)(2,1)} %copy-done.28, bf16[1024,3584]{1,0:T(8,128)(2,1)} %collective-permute-done.22.refs_3_, ...), custom_call_target="tpu_custom_call" | custom-call | flops 12884901888 | bytes 42949672 | tf_op jit(solution)/shard_map/pallas_call | solution.py:19
  822.6 34.4 %shard_map.196 = (f32[1024,4096]{1,0:T(8,128)}, f32[1024,2]{1,0:T(8,128)}) custom-call(bf16[4,192,4096]{2,1,0:T(8,128)(2,1)} %get-tuple-element.51.refs_0_, bf16[4,192,4096]{2,1,0:T(8,128)(2,1)} %collective-permute-done.14.refs_1_, s32[1024,4]{1,0:T(8,128)} %copy.101.refs_2_, f32[1024,2]{1,0:T(8,128)} %copy.104.refs_3_, bf16[1024,4096]{1,0:T(8,128)(2,1)} %refs_4_.5, ...), custom_call_target="tpu_custom_call" | custom-call | flops 25769803776 | bytes 85899344 | tf_op jit(solution)/shard_map/pallas_call | solution.py:19
  857.0 18.3 %shard_map.189.refs_1_.refs_3_.refs_11_ = bf16[4,384,4096]{2,1,0:T(8,128)(2,1)} custom-call(bf16[1024,4096]{1,0:T(8,128)(2,1)} %collective-permute-done.4.refs_0_, bf16[1024,4096]{1,0:T(8,128)(2,1)} %collective-permute-done.5.refs_1_, s32[768,2]{1,0:T(8,128)} %get-tuple-element.99.refs_2_.refs_4_), custom_call_target="tpu_custom_call" | custom-call | flops 12884901888 | bytes 42949672 | tf_op jit(solution)/shard_map/pallas_call | solution.py:19
  875.3 64.1 %shard_map.190 = (bf16[4,768,960]{2,1,0:T(8,128)(2,1)}, bf16[4,960,768]{2,1,0:T(8,128)(2,1)}, f32[4,768,960]{2,1,0:T(8,128)}, f32[4,768,960]{2,1,0:T(8,128)}) custom-call(bf16[4,384,4096]{2,1,0:T(8,128)(2,1)} %shard_map.188.refs_0_.refs_2_.refs_10_, bf16[4,384,4096]{2,1,0:T(8,128)(2,1)} %shard_map.189.refs_1_.refs_3_.refs_11_, ...), custom_call_target="tpu_custom_call" | custom-call | flops 48318382080 | bytes 161061280 | tf_op jit(solution)/shard_map/pallas_call | solution.py:19
  939.4 22.3 %shard_map.191 = (bf16[4,192,4096]{2,1,0:T(8,128)(2,1)}, bf16[4,192,4096]{2,1,0:T(8,128)(2,1)}) custom-call(bf16[4,768,960]{2,1,0:T(8,128)(2,1)} %get-tuple-element.45.refs_0_.refs_1_, bf16[4,768,960]{2,1,0:T(8,128)(2,1)} %get-tuple-element.45.refs_0_.refs_1_, bf16[4,960,4096]{2,1,0:T(8,128)(2,1)} %w_ref.3), custom_call_target="tpu_custom_call" | custom-call | flops 12079595520 | bytes 40265320 | tf_op jit(solution)/shard_map/pallas_call | solution.py:19
  963.6 45.7 %shard_map.200 = (bf16[4,768,960]{2,1,0:T(8,128)(2,1)}, bf16[4,768,960]{2,1,0:T(8,128)(2,1)}, bf16[4,960,768]{2,1,0:T(8,128)(2,1)}, bf16[4,960,768]{2,1,0:T(8,128)(2,1)}) custom-call(bf16[4,384,4096]{2,1,0:T(8,128)(2,1)} %shard_map.198.refs_0_.refs_3_, bf16[4,384,4096]{2,1,0:T(8,128)(2,1)} %shard_map.199.refs_1_.refs_4_, bf16[4,960,4096]{2,1,0:T(8,128)(2,1)} %w_ref.3, ...), custom_call_target="tpu_custom_call" | custom-call | flops 24159191040 | bytes 80530640 | tf_op jit(solution)/shard_map/pallas_call | solution.py:19
  1009.3 34.8 %shard_map.201 = (bf16[4,192,4096]{2,1,0:T(8,128)(2,1)}, bf16[4,192,4096]{2,1,0:T(8,128)(2,1)}) custom-call(bf16[4,768,960]{2,1,0:T(8,128)(2,1)} %get-tuple-element.58.refs_0_.refs_1_, bf16[4,768,960]{2,1,0:T(8,128)(2,1)} %get-tuple-element.58.refs_0_.refs_1_, bf16[4,768,960]{2,1,0:T(8,128)(2,1)} %get-tuple-element.59.refs_2_.refs_3_, ...), custom_call_target="tpu_custom_call" | custom-call | flops 24159191040 | bytes 80530640 | tf_op jit(solution)/shard_map/pallas_call | solution.py:19
  1044.8 11.2 shard_map.204.refs_0_.refs_13_
  1057.0 52.1 %shard_map.212.refs_16_ = f32[4,960,4096]{2,1,0:T(8,128)} custom-call(bf16[4,960,768]{2,1,0:T(8,128)(2,1)} %get-tuple-element.75.refs_0_, bf16[4,960,384]{2,1,0:T(8,128)(2,1)} %get-tuple-element.76.refs_1_, bf16[4,384,4096]{2,1,0:T(8,128)(2,1)} %shard_map.188.refs_0_.refs_2_.refs_10_, bf16[4,384,4096]{2,1,0:T(8,128)(2,1)} %shard_map.189.refs_1_.refs_3_.refs_11_, ...), custom_call_target="tpu_custom_call" | custom-call | flops 36238786560 | bytes 120795952 | tf_op jit(solution)/shard_map/pallas_call | solution.py:19
  1109.6 11.3 shard_map.208.q_ref.refs_4_
  1120.9 113.4 %collective-permute-done.9.refs_1_ = bf16[4,192,4096]{2,1,0:T(8,128)(2,1)} collective-permute-done((bf16[4,192,4096]{2,1,0:T(8,128)(2,1)}, bf16[4,192,4096]{2,1,0:T(8,128)(2,1)}, u32[]{:S(2)}, u32[]{:S(2)}) %collective-permute-start.9) | collective-permute-done | bytes 6291488 | tf_op jit(solution)/shard_map/ppermute | solution.py:393
  1234.4 34.5 %shard_map.197 = (bf16[1024,4096]{1,0:T(8,128)(2,1)}, f32[1024,2]{1,0:T(8,128)}) custom-call(bf16[4,192,4096]{2,1,0:T(8,128)(2,1)} %collective-permute-done.8.refs_0_, bf16[4,192,4096]{2,1,0:T(8,128)(2,1)} %collective-permute-done.9.refs_1_, s32[1024,4]{1,0:T(8,128)} %copy.103.refs_2_, f32[1024,2]{1,0:T(8,128)} %copy.104.refs_3_, ...), custom_call_target="tpu_custom_call" | custom-call | flops 25769803776 | bytes 85899344 | tf_op jit(solution)/shard_map/pallas_call | solution.py:19
  1268.9 1.8 multiply_reduce_fusion.1
  1270.7 2.0 add_convert_fusion.refs_7_
  1272.8 97.4 %collective-permute-done.23.refs_0_ = bf16[4,192,4096]{2,1,0:T(8,128)(2,1)} collective-permute-done((bf16[4,192,4096]{2,1,0:T(8,128)(2,1)}, bf16[4,192,4096]{2,1,0:T(8,128)(2,1)}, u32[]{:S(2)}, u32[]{:S(2)}) %collective-permute-start.23) | collective-permute-done | bytes 6291488 | tf_op jit(solution)/shard_map/ppermute | solution.py:393
  1370.1 133.9 %collective-permute-done.24.refs_1_ = bf16[4,192,4096]{2,1,0:T(8,128)(2,1)} collective-permute-done((bf16[4,192,4096]{2,1,0:T(8,128)(2,1)}, bf16[4,192,4096]{2,1,0:T(8,128)(2,1)}, u32[]{:S(2)}, u32[]{:S(2)}) %collective-permute-start.24) | collective-permute-done | bytes 6291488 | tf_op jit(solution)/shard_map/ppermute | solution.py:393
  1504.0 39.6 %shard_map.203 = (bf16[1024,4096]{1,0:T(8,128)(2,1)}, f32[1,4096]{1,0:T(1,128)}, f32[1,4096]{1,0:T(1,128)}) custom-call(bf16[4,192,4096]{2,1,0:T(8,128)(2,1)} %collective-permute-done.23.refs_0_, bf16[4,192,4096]{2,1,0:T(8,128)(2,1)} %collective-permute-done.24.refs_1_, s32[1024,4]{1,0:T(8,128)} %copy.103.refs_2_, f32[1024,4096]{1,0:T(8,128)} %shard_map.202.refs_3_, ...), custom_call_target="tpu_custom_call" | custom-call | flops 12884901888 | bytes 42949672 | tf_op jit(solution)/shard_map/pallas_call | solution.py:19
  1547.6 4.6 fusion.37
  1552.4 23.5 %shard_map.209.refs_5_.refs_2_ = f32[4,384,960]{2,1,0:T(8,128)} custom-call(bf16[4,384,4096]{2,1,0:T(8,128)(2,1)} %shard_map.208.q_ref.refs_4_, bf16[4,960,4096]{2,1,0:T(8,128)(2,1)} %w_ref.3), custom_call_target="tpu_custom_call" | custom-call | flops 12079595520 | bytes 40265320 | tf_op jit(solution)/shard_map/pallas_call | solution.py:19
  1579.4 4.8 shard_map.210.q_ref.refs_6_
  1585.9 6.6 collective-permute-done.35
  1593.7 6.2 collective-permute-done.36
  1600.7 10.7 shard_map.205.refs_1_.refs_14_
  1611.4 41.2 %shard_map.206 = (bf16[4,960,384]{2,1,0:T(8,128)(2,1)}, f32[4,384,960]{2,1,0:T(8,128)}, f32[4,384,960]{2,1,0:T(8,128)}) custom-call(bf16[4,192,4096]{2,1,0:T(8,128)(2,1)} %shard_map.204.refs_0_.refs_13_, bf16[4,192,4096]{2,1,0:T(8,128)(2,1)} %shard_map.205.refs_1_.refs_14_, bf16[4,960,4096]{2,1,0:T(8,128)(2,1)} %bitcast.91, bf16[4,960,4096]{2,1,0:T(8,128)(2,1)} %bitcast.96), custom_call_target="tpu_custom_call" | custom-call | flops 24159191040 | bytes 80530640 | tf_op jit(solution)/shard_map/pallas_call | solution.py:19
  1652.6 13.6 shard_map.211
  1666.3 143.6 %shard_map.213 = (f32[4,960,4096]{2,1,0:T(8,128)}, f32[4,960,4096]{2,1,0:T(8,128)}, f32[4,960,4096]{2,1,0:T(8,128)}) custom-call(bf16[4,960,768]{2,1,0:T(8,128)(2,1)} %get-tuple-element.66.refs_0_, bf16[4,960,384]{2,1,0:T(8,128)(2,1)} %get-tuple-element.67.refs_1_, bf16[4,960,384]{2,1,0:T(8,128)(2,1)} %get-tuple-element.68.refs_2_, ...), custom_call_target="tpu_custom_call", output_to_operand_aliasing={{2}: (16, {})} | custom-call | flops 108716359680 | bytes 362387872 | tf_op jit(solution)/shard_map/pallas_call | solution.py:19
  (195 shorter events, 51.5 us)
Async XLA Ops:
  7.7 174.8 %collective-permute-start.13 = (bf16[1024,3584]{1,0:T(8,128)(2,1)}, bf16[1024,3584]{1,0:T(8,128)(2,1)}, u32[]{:S(2)}, u32[]{:S(2)}) collective-permute-start(bf16[1024,3584]{1,0:T(8,128)(2,1)} %slice.67.refs_1_), channel_id=1, source_target_pairs={{0,1},{1,0},{2,3},{3,2},{4,5},{5,4},{6,7},{7,6}} | collective-permute-start | bytes 22020104 | tf_op jit(solution)/shard_map/ppermute | solution.py:393
  18.3 188.3 %collective-permute-start.10 = (bf16[1024,4096]{1,0:T(8,128)(2,1)}, bf16[1024,4096]{1,0:T(8,128)(2,1)}, u32[]{:S(2)}, u32[]{:S(2)}) collective-permute-start(bf16[1024,4096]{1,0:T(8,128)(2,1)} %fusion.5.refs_0_), channel_id=1, source_target_pairs={{0,1},{1,0},{2,3},{3,2},{4,5},{5,4},{6,7},{7,6}} | collective-permute-start | bytes 25165832 | tf_op jit(solution)/shard_map/ppermute | solution.py:393
  18.6 269.6 %collective-permute-start.16 = (bf16[1024,3584]{1,0:T(8,128)(2,1)}, bf16[1024,3584]{1,0:T(8,128)(2,1)}, u32[]{:S(2)}, u32[]{:S(2)}) collective-permute-start(bf16[1024,3584]{1,0:T(8,128)(2,1)} %slice.67.refs_1_), channel_id=1, source_target_pairs={{0,2},{1,3},{2,0},{3,1},{4,6},{5,7},{6,4},{7,5}} | collective-permute-start | bytes 22020104 | tf_op jit(solution)/shard_map/ppermute | solution.py:393
  22.6 157.8 %copy-start.10 = (bf16[1024,512]{1,0:T(8,128)(2,1)}, bf16[1024,512]{1,0:T(8,128)(2,1)S(1)}, u32[]{:S(2)}) copy-start(bf16[1024,512]{1,0:T(8,128)(2,1)S(1)} %slice.66.refs_0_) | copy-start | bytes 3145732
  22.7 159.6 %collective-permute-start.12 = (bf16[1024,512]{1,0:T(8,128)(2,1)S(1)}, bf16[1024,512]{1,0:T(8,128)(2,1)}, u32[]{:S(2)}, u32[]{:S(2)}) collective-permute-start(bf16[1024,512]{1,0:T(8,128)(2,1)S(1)} %slice.66.refs_0_), channel_id=1, source_target_pairs={{0,1},{1,0},{2,3},{3,2},{4,5},{5,4},{6,7},{7,6}} | collective-permute-start | bytes 3145736 | tf_op jit(solution)/shard_map/ppermute | solution.py:393
  41.5 1.3 collective-permute-start.11
  42.7 137.8 %collective-permute-start.2 = (f32[2,3072]{1,0:T(2,128)S(1)}, f32[2,3072]{1,0:T(2,128)S(1)}, u32[]{:S(2)}, u32[]{:S(2)}) collective-permute-start(f32[2,3072]{1,0:T(2,128)S(1)} %pad_maximum_fusion.5), channel_id=1, source_target_pairs={{0,2},{1,3},{2,0},{3,1},{4,6},{5,7},{6,4},{7,5}} | collective-permute-start | bytes 73736 | tf_op jit(solution)/shard_map/ppermute | solution.py:393
  180.5 48.2 %collective-permute-start.17 = (bf16[1024,512]{1,0:T(8,128)(2,1)S(1)}, bf16[1024,512]{1,0:T(8,128)(2,1)S(1)}, u32[]{:S(2)}, u32[]{:S(2)}) collective-permute-start(bf16[1024,512]{1,0:T(8,128)(2,1)S(1)} %slice.66.refs_0_), channel_id=1, source_target_pairs={{0,4},{1,5},{2,6},{3,7},{4,0},{5,1},{6,2},{7,3}} | collective-permute-start | bytes 3145736 | tf_op jit(solution)/shard_map/ppermute | solution.py:393
  182.3 23.9 %collective-permute-start.3 = (f32[2,3072]{1,0:T(2,128)S(1)}, f32[2,3072]{1,0:T(2,128)S(1)}, u32[]{:S(2)}, u32[]{:S(2)}) collective-permute-start(f32[2,3072]{1,0:T(2,128)S(1)} %pad_maximum_fusion.5), channel_id=1, source_target_pairs={{0,4},{1,5},{2,6},{3,7},{4,0},{5,1},{6,2},{7,3}} | collective-permute-start | bytes 73736 | tf_op jit(solution)/shard_map/ppermute | solution.py:393
  182.5 23.9 %collective-permute-start.27 = (f32[2,3072]{1,0:T(2,128)S(1)}, f32[2,3072]{1,0:T(2,128)S(1)}, u32[]{:S(2)}, u32[]{:S(2)}) collective-permute-start(f32[2,3072]{1,0:T(2,128)S(1)} %collective-permute-done.2), channel_id=1, source_target_pairs={{0,4},{1,5},{2,6},{3,7},{4,0},{5,1},{6,2},{7,3}} | collective-permute-start | bytes 73736 | tf_op jit(solution)/shard_map/ppermute | solution.py:393
  206.1 20.6 %collective-permute-start.6 = (f32[2,3072]{1,0:T(2,128)S(1)}, f32[2,3072]{1,0:T(2,128)S(1)}, u32[]{:S(2)}, u32[]{:S(2)}) collective-permute-start(f32[2,3072]{1,0:T(2,128)S(1)} %collective-permute-done.2), channel_id=1, source_target_pairs={{0,1},{1,0},{2,3},{3,2},{4,5},{5,4},{6,7},{7,6}} | collective-permute-start | bytes 73736 | tf_op jit(solution)/shard_map/ppermute | solution.py:393
  206.4 18.8 %collective-permute-start.7 = (f32[2,3072]{1,0:T(2,128)S(1)}, f32[2,3072]{1,0:T(2,128)S(1)}, u32[]{:S(2)}, u32[]{:S(2)}) collective-permute-start(f32[2,3072]{1,0:T(2,128)S(1)} %collective-permute-done.3), channel_id=1, source_target_pairs={{0,1},{1,0},{2,3},{3,2},{4,5},{5,4},{6,7},{7,6}} | collective-permute-start | bytes 73736 | tf_op jit(solution)/shard_map/ppermute | solution.py:393
  206.6 21.6 %collective-permute-start.29 = (f32[2,3072]{1,0:T(2,128)S(1)}, f32[2,3072]{1,0:T(2,128)S(1)}, u32[]{:S(2)}, u32[]{:S(2)}) collective-permute-start(f32[2,3072]{1,0:T(2,128)S(1)} %collective-permute-done.27), channel_id=1, source_target_pairs={{0,1},{1,0},{2,3},{3,2},{4,5},{5,4},{6,7},{7,6}} | collective-permute-start | bytes 73736 | tf_op jit(solution)/shard_map/ppermute | solution.py:393
  225.2 62.5 %collective-permute-start.15 = (bf16[1024,512]{1,0:T(8,128)(2,1)S(1)}, bf16[1024,512]{1,0:T(8,128)(2,1)}, u32[]{:S(2)}, u32[]{:S(2)}) collective-permute-start(bf16[1024,512]{1,0:T(8,128)(2,1)S(1)} %copy-done.11), channel_id=1, source_target_pairs={{0,2},{1,3},{2,0},{3,1},{4,6},{5,7},{6,4},{7,5}} | collective-permute-start | bytes 3145736 | tf_op jit(solution)/shard_map/ppermute | solution.py:393
  226.7 161.2 %collective-permute-start.18 = (bf16[1024,3584]{1,0:T(8,128)(2,1)}, bf16[1024,3584]{1,0:T(8,128)(2,1)}, u32[]{:S(2)}, u32[]{:S(2)}) collective-permute-start(bf16[1024,3584]{1,0:T(8,128)(2,1)} %slice.67.refs_1_), channel_id=1, source_target_pairs={{0,4},{1,5},{2,6},{3,7},{4,0},{5,1},{6,2},{7,3}} | collective-permute-start | bytes 22020104 | tf_op jit(solution)/shard_map/ppermute | solution.py:393
  228.2 339.4 %collective-permute-start.1 = (bf16[1024,4096]{1,0:T(8,128)(2,1)}, bf16[1024,4096]{1,0:T(8,128)(2,1)}, u32[]{:S(2)}, u32[]{:S(2)}) collective-permute-start(bf16[1024,4096]{1,0:T(8,128)(2,1)} %fusion.5.refs_0_), channel_id=1, source_target_pairs={{0,4},{1,5},{2,6},{3,7},{4,0},{5,1},{6,2},{7,3}} | collective-permute-start | bytes 25165832 | tf_op jit(solution)/shard_map/ppermute | solution.py:393
  228.7 58.9 %copy-start.27 = (bf16[1024,512]{1,0:T(8,128)(2,1)}, bf16[1024,512]{1,0:T(8,128)(2,1)S(1)}, u32[]{:S(2)}) copy-start(bf16[1024,512]{1,0:T(8,128)(2,1)S(1)} %collective-permute-done.17.refs_2_) | copy-start | bytes 3145732
  228.7 59.5 %collective-permute-start.21 = (bf16[1024,512]{1,0:T(8,128)(2,1)S(1)}, bf16[1024,512]{1,0:T(8,128)(2,1)S(1)}, u32[]{:S(2)}, u32[]{:S(2)}) collective-permute-start(bf16[1024,512]{1,0:T(8,128)(2,1)S(1)} %collective-permute-done.17.refs_2_), channel_id=1, source_target_pairs={{0,1},{1,0},{2,3},{3,2},{4,5},{5,4},{6,7},{7,6}} | collective-permute-start | bytes 3145736 | tf_op jit(solution)/shard_map/ppermute | solution.py:393
  287.7 288.7 %collective-permute-start = (bf16[1024,4096]{1,0:T(8,128)(2,1)}, bf16[1024,4096]{1,0:T(8,128)(2,1)}, u32[]{:S(2)}, u32[]{:S(2)}) collective-permute-start(bf16[1024,4096]{1,0:T(8,128)(2,1)} %fusion.5.refs_0_), channel_id=1, source_target_pairs={{0,2},{1,3},{2,0},{3,1},{4,6},{5,7},{6,4},{7,5}} | collective-permute-start | bytes 25165832 | tf_op jit(solution)/shard_map/ppermute | solution.py:393
  288.2 53.0 %copy-start.28 = (bf16[1024,512]{1,0:T(8,128)(2,1)}, bf16[1024,512]{1,0:T(8,128)(2,1)S(1)}, u32[]{:S(2)}) copy-start(bf16[1024,512]{1,0:T(8,128)(2,1)S(1)} %collective-permute-done.21.refs_2_) | copy-start | bytes 3145732
  288.2 53.0 %collective-permute-start.19 = (bf16[1024,512]{1,0:T(8,128)(2,1)}, bf16[1024,512]{1,0:T(8,128)(2,1)S(1)}, u32[]{:S(2)}, u32[]{:S(2)}) collective-permute-start(bf16[1024,512]{1,0:T(8,128)(2,1)} %collective-permute-done.15.refs_0_), channel_id=1, source_target_pairs={{0,1},{1,0},{2,3},{3,2},{4,5},{5,4},{6,7},{7,6}} | collective-permute-start | bytes 3145736 | tf_op jit(solution)/shard_map/ppermute | solution.py:393
  288.3 435.7 %collective-permute-start.32 = (bf16[1024,3584]{1,0:T(8,128)(2,1)}, bf16[1024,3584]{1,0:T(8,128)(2,1)}, u32[]{:S(2)}, u32[]{:S(2)}) collective-permute-start(bf16[1024,3584]{1,0:T(8,128)(2,1)} %collective-permute-done.16.refs_1_), channel_id=1, source_target_pairs={{0,4},{1,5},{2,6},{3,7},{4,0},{5,1},{6,2},{7,3}} | collective-permute-start | bytes 22020104 | tf_op jit(solution)/shard_map/ppermute | solution.py:393
  341.3 390.6 %copy-start.29 = (bf16[1024,512]{1,0:T(8,128)(2,1)}, bf16[1024,512]{1,0:T(8,128)(2,1)S(1)}, u32[]{:S(2)}) copy-start(bf16[1024,512]{1,0:T(8,128)(2,1)S(1)} %collective-permute-done.19.refs_0_) | copy-start | bytes 3145732
  341.3 382.6 %collective-permute-start.25 = (bf16[4,192,4096]{2,1,0:T(8,128)(2,1)}, bf16[4,192,4096]{2,1,0:T(8,128)(2,1)}, u32[]{:S(2)}, u32[]{:S(2)}) collective-permute-start(bf16[4,192,4096]{2,1,0:T(8,128)(2,1)} %get-tuple-element.63), channel_id=1, source_target_pairs={{0,1},{1,0},{2,3},{3,2},{4,5},{5,4},{6,7},{7,6}} | collective-permute-start | bytes 18874376 | tf_op jit(solution)/shard_map/ppermute | solution.py:393
  387.9 413.0 %collective-permute-start.22 = (bf16[1024,3584]{1,0:T(8,128)(2,1)}, bf16[1024,3584]{1,0:T(8,128)(2,1)}, u32[]{:S(2)}, u32[]{:S(2)}) collective-permute-start(bf16[1024,3584]{1,0:T(8,128)(2,1)} %collective-permute-done.18.refs_3_), channel_id=1, source_target_pairs={{0,1},{1,0},{2,3},{3,2},{4,5},{5,4},{6,7},{7,6}} | collective-permute-start | bytes 22020104 | tf_op jit(solution)/shard_map/ppermute | solution.py:393
  567.6 234.7 %collective-permute-start.20 = (bf16[1024,3584]{1,0:T(8,128)(2,1)}, bf16[1024,3584]{1,0:T(8,128)(2,1)}, u32[]{:S(2)}, u32[]{:S(2)}) collective-permute-start(bf16[1024,3584]{1,0:T(8,128)(2,1)} %collective-permute-done.16.refs_1_), channel_id=1, source_target_pairs={{0,1},{1,0},{2,3},{3,2},{4,5},{5,4},{6,7},{7,6}} | collective-permute-start | bytes 22020104 | tf_op jit(solution)/shard_map/ppermute | solution.py:393
  576.3 246.3 %collective-permute-start.14 = (bf16[4,192,4096]{2,1,0:T(8,128)(2,1)}, bf16[4,192,4096]{2,1,0:T(8,128)(2,1)}, u32[]{:S(2)}, u32[]{:S(2)}) collective-permute-start(bf16[4,192,4096]{2,1,0:T(8,128)(2,1)} %get-tuple-element.52), channel_id=1, source_target_pairs={{0,1},{1,0},{2,3},{3,2},{4,5},{5,4},{6,7},{7,6}} | collective-permute-start | bytes 18874376 | tf_op jit(solution)/shard_map/ppermute | solution.py:393
  723.9 133.1 %collective-permute-start.5 = (bf16[1024,4096]{1,0:T(8,128)(2,1)}, bf16[1024,4096]{1,0:T(8,128)(2,1)}, u32[]{:S(2)}, u32[]{:S(2)}) collective-permute-start(bf16[1024,4096]{1,0:T(8,128)(2,1)} %collective-permute-done.1.refs_1_), channel_id=1, source_target_pairs={{0,1},{1,0},{2,3},{3,2},{4,5},{5,4},{6,7},{7,6}} | collective-permute-start | bytes 25165832 | tf_op jit(solution)/shard_map/ppermute | solution.py:393
  723.9 133.1 %collective-permute-start.4 = (bf16[1024,4096]{1,0:T(8,128)(2,1)}, bf16[1024,4096]{1,0:T(8,128)(2,1)}, u32[]{:S(2)}, u32[]{:S(2)}) collective-permute-start(bf16[1024,4096]{1,0:T(8,128)(2,1)} %collective-permute-done.refs_0_), channel_id=1, source_target_pairs={{0,1},{1,0},{2,3},{3,2},{4,5},{5,4},{6,7},{7,6}} | collective-permute-start | bytes 25165832 | tf_op jit(solution)/shard_map/ppermute | solution.py:393
  800.8 255.1 %collective-permute-start.30 = (bf16[1024,512]{1,0:T(8,128)(2,1)}, bf16[1024,512]{1,0:T(8,128)(2,1)}, u32[]{:S(2)}, u32[]{:S(2)}) collective-permute-start(bf16[1024,512]{1,0:T(8,128)(2,1)} %collective-permute-done.15.refs_0_), channel_id=1, source_target_pairs={{0,4},{1,5},{2,6},{3,7},{4,0},{5,1},{6,2},{7,3}} | collective-permute-start | bytes 3145736 | tf_op jit(solution)/shard_map/ppermute | solution.py:393
  802.3 241.8 %collective-permute-start.26 = (bf16[1024,4096]{1,0:T(8,128)(2,1)}, bf16[1024,4096]{1,0:T(8,128)(2,1)}, u32[]{:S(2)}, u32[]{:S(2)}) collective-permute-start(bf16[1024,4096]{1,0:T(8,128)(2,1)} %collective-permute-done.refs_0_), channel_id=1, source_target_pairs={{0,4},{1,5},{2,6},{3,7},{4,0},{5,1},{6,2},{7,3}} | collective-permute-start | bytes 25165832 | tf_op jit(solution)/shard_map/ppermute | solution.py:393
  822.6 286.5 %collective-permute-start.33 = (bf16[1024,3584]{1,0:T(8,128)(2,1)}, bf16[1024,3584]{1,0:T(8,128)(2,1)}, u32[]{:S(2)}, u32[]{:S(2)}) collective-permute-start(bf16[1024,3584]{1,0:T(8,128)(2,1)} %collective-permute-done.32.refs_0_), channel_id=1, source_target_pairs={{0,1},{1,0},{2,3},{3,2},{4,5},{5,4},{6,7},{7,6}} | collective-permute-start | bytes 22020104 | tf_op jit(solution)/shard_map/ppermute | solution.py:393
  961.8 159.1 %collective-permute-start.8 = (bf16[4,192,4096]{2,1,0:T(8,128)(2,1)}, bf16[4,192,4096]{2,1,0:T(8,128)(2,1)}, u32[]{:S(2)}, u32[]{:S(2)}) collective-permute-start(bf16[4,192,4096]{2,1,0:T(8,128)(2,1)} %get-tuple-element.46), channel_id=1, source_target_pairs={{0,2},{1,3},{2,0},{3,1},{4,6},{5,7},{6,4},{7,5}} | collective-permute-start | bytes 18874376 | tf_op jit(solution)/shard_map/ppermute | solution.py:393
  962.4 272.0 %collective-permute-start.9 = (bf16[4,192,4096]{2,1,0:T(8,128)(2,1)}, bf16[4,192,4096]{2,1,0:T(8,128)(2,1)}, u32[]{:S(2)}, u32[]{:S(2)}) collective-permute-start(bf16[4,192,4096]{2,1,0:T(8,128)(2,1)} %get-tuple-element.47), channel_id=1, source_target_pairs={{0,3},{1,2},{2,1},{3,0},{4,7},{5,6},{6,5},{7,4}} | collective-permute-start | bytes 18874376 | tf_op jit(solution)/shard_map/ppermute | solution.py:393
  1044.2 326.0 %collective-permute-start.23 = (bf16[4,192,4096]{2,1,0:T(8,128)(2,1)}, bf16[4,192,4096]{2,1,0:T(8,128)(2,1)}, u32[]{:S(2)}, u32[]{:S(2)}) collective-permute-start(bf16[4,192,4096]{2,1,0:T(8,128)(2,1)} %get-tuple-element.60), channel_id=1, source_target_pairs={{0,2},{1,3},{2,0},{3,1},{4,6},{5,7},{6,4},{7,5}} | collective-permute-start | bytes 18874376 | tf_op jit(solution)/shard_map/ppermute | solution.py:393
  1055.9 448.1 %collective-permute-start.24 = (bf16[4,192,4096]{2,1,0:T(8,128)(2,1)}, bf16[4,192,4096]{2,1,0:T(8,128)(2,1)}, u32[]{:S(2)}, u32[]{:S(2)}) collective-permute-start(bf16[4,192,4096]{2,1,0:T(8,128)(2,1)} %get-tuple-element.61), channel_id=1, source_target_pairs={{0,3},{1,2},{2,1},{3,0},{4,7},{5,6},{6,5},{7,4}} | collective-permute-start | bytes 18874376 | tf_op jit(solution)/shard_map/ppermute | solution.py:393
  1109.1 443.1 %collective-permute-start.31 = (bf16[1024,512]{1,0:T(8,128)(2,1)}, bf16[1024,512]{1,0:T(8,128)(2,1)S(1)}, u32[]{:S(2)}, u32[]{:S(2)}) collective-permute-start(bf16[1024,512]{1,0:T(8,128)(2,1)} %collective-permute-done.30.refs_0_), channel_id=1, source_target_pairs={{0,1},{1,0},{2,3},{3,2},{4,5},{5,4},{6,7},{7,6}} | collective-permute-start | bytes 3145736 | tf_op jit(solution)/shard_map/ppermute | solution.py:393
  1120.9 479.8 %collective-permute-start.28 = (bf16[1024,4096]{1,0:T(8,128)(2,1)}, bf16[1024,4096]{1,0:T(8,128)(2,1)}, u32[]{:S(2)}, u32[]{:S(2)}) collective-permute-start(bf16[1024,4096]{1,0:T(8,128)(2,1)} %collective-permute-done.26.refs_0_), channel_id=1, source_target_pairs={{0,1},{1,0},{2,3},{3,2},{4,5},{5,4},{6,7},{7,6}} | collective-permute-start | bytes 25165832 | tf_op jit(solution)/shard_map/ppermute | solution.py:393
  1544.4 31.5 %collective-permute-start.42 = (f32[2,4096]{1,0:T(2,128)S(1)}, f32[2,4096]{1,0:T(2,128)S(1)}, u32[]{:S(2)}, u32[]{:S(2)}) collective-permute-start(f32[2,4096]{1,0:T(2,128)S(1)} %pad_maximum_fusion.4), channel_id=1, source_target_pairs={{0,6},{1,7},{2,4},{3,5},{4,2},{5,3},{6,0},{7,1}} | collective-permute-start | bytes 98312 | tf_op jit(solution)/shard_map/ppermute | solution.py:393
  1545.9 31.4 %collective-permute-start.41 = (f32[2,4096]{1,0:T(2,128)S(1)}, f32[2,4096]{1,0:T(2,128)S(1)}, u32[]{:S(2)}, u32[]{:S(2)}) collective-permute-start(f32[2,4096]{1,0:T(2,128)S(1)} %pad_maximum_fusion.4), channel_id=1, source_target_pairs={{0,5},{1,4},{2,7},{3,6},{4,1},{5,0},{6,3},{7,2}} | collective-permute-start | bytes 98312 | tf_op jit(solution)/shard_map/ppermute | solution.py:393
  1546.1 31.7 %collective-permute-start.40 = (f32[2,4096]{1,0:T(2,128)S(1)}, f32[2,4096]{1,0:T(2,128)S(1)}, u32[]{:S(2)}, u32[]{:S(2)}) collective-permute-start(f32[2,4096]{1,0:T(2,128)S(1)} %pad_maximum_fusion.4), channel_id=1, source_target_pairs={{0,4},{1,5},{2,6},{3,7},{4,0},{5,1},{6,2},{7,3}} | collective-permute-start | bytes 98312 | tf_op jit(solution)/shard_map/ppermute | solution.py:393
  1552.2 26.7 %collective-permute-start.34 = (f32[16,4096]{1,0:T(8,128)S(1)}, f32[16,4096]{1,0:T(8,128)S(1)}, u32[]{:S(2)}, u32[]{:S(2)}) collective-permute-start(f32[16,4096]{1,0:T(8,128)S(1)} %fusion.37), channel_id=1, source_target_pairs={{0,1},{1,0},{2,3},{3,2},{4,5},{5,4},{6,7},{7,6}} | collective-permute-start | bytes 786440 | tf_op jit(solution)/shard_map/ppermute | solution.py:393
  1576.0 8.3 collective-permute-start.39
  1577.3 8.5 collective-permute-start.38
  1577.8 8.0 collective-permute-start.43
  1578.9 6.9 collective-permute-start.37
  1584.2 8.3 collective-permute-start.35
  1592.5 7.4 collective-permute-start.36
  (27 other events, 537.5 us)
